TPU v7x, 32 devices: a whole 2x2x4 slice. The times are simulated.
32 devices in a mesh: gx: 2 (over x), gy: 4 (over y, core), gz: 4 (over z).
Axes of the slice: x: 2, y: 2, z: 4, core: 2. Of those that a mesh axis runs over, the one named last changes fastest.
Arguments:
- fields: float32 [6, 32, 64, 512], P(None, 'gx', 'gy', 'gz'), may hold values from -6 to 6
- permittivity: float32 [32, 64, 512], P('gx', 'gy', 'gz'), may hold values from 1 to 4
- donor_owner: int32 [4096, 1], P(('gx', 'gy', 'gz')), may hold values from 0 to 15; in each aligned block of 128 rows (0 to 127, 128 to 255, ...) at most 16 rows name the same one
- donor_base: int32 [4096, 3], P(('gx', 'gy', 'gz')), may hold values from 0 to 127, as said below
- donor_weights: float32 [4096, 15], P(('gx', 'gy', 'gz')), may hold values from -3 to 3
Outputs:
- new_fields: float32 [6, 32, 64, 512], P(None, 'gx', 'gy', 'gz')
- receptor_values: float32 [6, 4096], P(None, ('gx', 'gy', 'gz'))
Inputs may be any that keep to these rules, and one draw needn't show every extreme that they name: `donor_owner`: within the 128 rows of one device no owner index is named by more than 16 rows, and one is named by exactly 16. `donor_base`: column 0 lies in 0 to 15, column 1 in 0 to 15, column 2 in 0 to 127.
All inputs are finite; a program needn't handle non-finite values.
Results may differ from a plain program's by a relative error of at most 0.00002.
Values sent between devices are 32-bit elements; how exact they have to be, the bound alone decides.
A program may use at most 192 MiB of HBM per device.

v0:
```python
import functools

import jax
import jax.numpy as jnp
from jax import lax
from jax.experimental import pallas as pl
from jax.experimental.pallas import tpu as pltpu
from jax.sharding import PartitionSpec as P

step_size = 0.25
MESH = pl.DeviceIdType.MESH
Y_COMPS = (0, 2, 3, 5)
Z_COMPS = (0, 1, 3, 4)
F32 = jnp.float32
HI = lax.Precision.HIGHEST


def dot(a, b, dims=((1,), (0,))):
    return lax.dot_general(a, b, (dims, ((), ())), precision=HI, preferred_element_type=F32)


def split(a):
    hi = a.astype(jnp.bfloat16)
    return hi, (a - hi.astype(F32)).astype(jnp.bfloat16)


def dot16(a, b):
    return lax.dot_general(a, b, (((1,), (0,)), ((), ())), preferred_element_type=F32)


def kernel(
    sizes, fields, eps, owner, bases, weights, out, recept,
    T, F, H, inv, ys, yr, zs, zr, yfs, yfr, zfs, zfr,
    zfd, DZ, E, data_t, inner, outer, req, reqr, ans, ansr, W, W_lo, wz_in, wz_halo, perm,
    load_sem, send, recv, fsend, frecv, rsend, rrecv, asend, arecv, dsend, drecv,
):
    nx, ny, nz, cap = sizes
    group = ny * nz
    cx, cy, cz = eps.shape
    x, y, z = lax.axis_index("gx"), lax.axis_index("gy"), lax.axis_index("gz")
    me = y * nz + z
    y0, y1 = 8, 8 + cy

    loads = [
        pltpu.make_async_copy(fields, T.at[0, :, pl.ds(2, cx), pl.ds(8, cy), :], load_sem.at[0]),
        pltpu.make_async_copy(fields, F.at[:, pl.ds(2, cx), pl.ds(8, cy), :], load_sem.at[1]),
        pltpu.make_async_copy(eps, inv, load_sem.at[2]),
    ]
    for copy in loads:
        copy.start()

    def clear(ref):
        ref[...] = jnp.zeros(ref.shape, F32)

    for m in range(4):
        for lo in (0, cx + 2):
            clear(T.at[m, :, pl.ds(lo, 2)])
    for lo in (0, cx + 2):
        clear(F.at[:, pl.ds(lo, 2)])
        clear(H.at[pl.ds(lo, 2)])
    for lo in (0, y1):
        clear(F.at[:, pl.ds(2, cx), pl.ds(lo, 8)])
        clear(H.at[pl.ds(2, cx), pl.ds(lo, 8)])
    for ref in (yr, zr, yfr, zfr, zfd):
        clear(ref)

    barrier = pltpu.get_barrier_semaphore()
    others = []
    for d in range(1, group):
        t = lax.rem(me + d, group)
        others.append((x, t // nz, lax.rem(t, nz)))
    for target in others:
        pl.semaphore_signal(barrier, inc=1, device_id=target, device_id_type=MESH)

    has = {"xl": x > 0, "xh": x < nx - 1, "yl": y > 0, "yh": y < ny - 1, "zl": z > 0, "zh": z < nz - 1}
    dev = {
        "xl": (x - 1, y, z), "xh": (x + 1, y, z), "yl": (x, y - 1, z), "yh": (x, y + 1, z),
        "zl": (x, y, z - 1), "zh": (x, y, z + 1),
    }
    for side in ("xl", "xh"):
        @pl.when(has[side])
        def _():
            pl.semaphore_signal(barrier, inc=1, device_id=dev[side], device_id_type=MESH)

    corners = [(sx, sz) for sx in ("xl", "xh") for sz in ("zl", "zh")]

    def corner_dev(sx, sz):
        return (dev[sx][0], y, dev[sz][2])

    expected = group - 1 + has["xl"].astype(jnp.int32) + has["xh"].astype(jnp.int32)
    for sx, sz in corners:
        both = has[sx] & has[sz]
        expected = expected + both.astype(jnp.int32)

        @pl.when(both)
        def _():
            pl.semaphore_signal(barrier, inc=1, device_id=corner_dev(sx, sz), device_id_type=MESH)

    rows = owner.shape[1]
    data_t[...] = jnp.zeros(data_t.shape, F32)
    data_t[0:3] = bases[...].astype(F32)
    data_t[3:18] = weights[...]
    data_t[18:19] = owner[...].astype(F32)
    data = jnp.transpose(data_t[...])
    col = lax.broadcasted_iota(jnp.int32, (rows, 128), 1)
    own = data[:, 18:19].astype(jnp.int32)
    hits = (own == col).astype(F32)
    earlier = dot((lax.broadcasted_iota(jnp.int32, (rows, rows), 1)
                   < lax.broadcasted_iota(jnp.int32, (rows, rows), 0)).astype(F32), hits)
    slot = jnp.sum(earlier * hits, axis=1, keepdims=True).astype(jnp.int32)
    flat = own * cap + slot
    slots = group * cap
    perm[...] = (flat == lax.broadcasted_iota(jnp.int32, (rows, slots), 1)).astype(F32)
    packed = dot(perm[...], data, ((0,), (0,)))
    for o in range(group):
        req[o] = packed[o * cap:(o + 1) * cap]
    reqr[me] = req[me]

    for copy in loads:
        copy.wait()
    inv[...] = 1.0 / (12.0 * inv[...])

    zi = lax.broadcasted_iota(jnp.int32, (cz, cz), 0)
    zo = lax.broadcasted_iota(jnp.int32, (cz, cz), 1)

    def stencil(delta):
        return (jnp.where(delta == -2, 1.0, 0.0) - jnp.where(delta == 2, 1.0, 0.0)
                + jnp.where(delta == 1, 8.0, 0.0) - jnp.where(delta == -1, 8.0, 0.0))

    inner[...] = stencil(zi - zo).astype(jnp.bfloat16)
    outer[...] = (stencil(zi - cz - zo) * jnp.where(zi >= cz // 2, 1.0, 0.0)
                  + stencil(zi + cz - zo) * jnp.where(zi < cz // 2, 1.0, 0.0)).astype(jnp.bfloat16)

    pl.semaphore_wait(barrier, expected)

    def remote(src, dst, s, r, target):
        return pltpu.make_async_remote_copy(
            src_ref=src, dst_ref=dst, send_sem=s, recv_sem=r, device_id=target, device_id_type=MESH)

    def request(d):
        return remote(req.at[(me + d) % group], reqr.at[me], rsend.at[d], rrecv.at[d], others[d - 1])

    def answer(d):
        return remote(ans.at[(me + d) % group], ansr.at[me], asend.at[d], arecv.at[d], others[d - 1])

    lane = lax.broadcasted_iota(jnp.int32, (cy, cz), 1)
    opposite = {"xl": "xh", "xh": "xl", "yl": "yh", "yh": "yl", "zl": "zh", "zh": "zl"}

    def x_copies(m, side):
        lo_src, lo_dst = (2, cx + 2) if side == "xl" else (cx, 0)
        base = 0 if side == "xl" else 2
        return [
            remote(T.at[m, pl.ds(c, 2), pl.ds(lo_src, 2), pl.ds(8, cy)],
                   T.at[m, pl.ds(c, 2), pl.ds(lo_dst, 2), pl.ds(8, cy)],
                   send.at[m, base + i], recv.at[m, base + i], dev[side])
            for i, c in enumerate((1, 4))
        ]

    def y_copies(m, side):
        k = 0 if side == "yl" else 1
        return [remote(ys.at[m, k], yr.at[m, k], send.at[m, 4 + k], recv.at[m, 4 + k], dev[side])]

    def z_copies(m, side):
        k = 0 if side == "zl" else 1
        return [remote(zs.at[m], zr.at[m, k], send.at[m, 6 + k], recv.at[m, 6 + k], dev[side])]

    def start(copies, side):
        @pl.when(has[side])
        def _():
            for copy in copies:
                copy.start()

    def finish_recv(copies, side):
        @pl.when(has[opposite[side]])
        def _():
            for copy in copies:
                copy.wait_recv()

    def finish_send(copies, side):
        @pl.when(has[side])
        def _():
            for copy in copies:
                copy.wait_send()

    per = cz // 16

    def step(m, carry):
        for side in ("xl", "xh"):
            start(x_copies(m, side), side)

        def pack(g, c_):
            strip = jnp.zeros((cy, cz), F32)
            for i in range(per):
                px = 2 + g * per + i
                for q, c in enumerate(Z_COMPS):
                    b = (i * 4 + q) * 4
                    strip = jnp.where(lane // 4 == i * 4 + q,
                                      pltpu.roll(T[m, c, px, y0:y1, :], (b + 2) % cz, 1), strip)
            zs[m, g] = strip
            return c_

        lax.fori_loop(0, cx // per, pack, 0)
        for side in ("zl", "zh"):
            start(z_copies(m, side), side)
        for q, c in enumerate(Y_COMPS):
            ys[m, 0, :, 2 * q:2 * q + 2, :] = T[m, c, 2:2 + cx, y0:y0 + 2, :]
            ys[m, 1, :, 2 * q:2 * q + 2, :] = T[m, c, 2:2 + cx, y1 - 2:y1, :]
        for side in ("yl", "yh"):
            start(y_copies(m, side), side)

        @pl.when(m == 0)
        def _():
            for d in range(1, group):
                request(d).start()

        for q, c in enumerate(Z_COMPS):
            hi, lo = split(T[m, c, 2:2 + cx, y0:y1, :].reshape(cx * cy, cz))
            DZ[q] = (dot16(hi, inner[...]) + dot16(lo, inner[...])).reshape(cx, cy, cz)

        for side in ("zl", "zh"):
            finish_recv(z_copies(m, side), side)
        for side in ("yl", "yh"):
            finish_recv(y_copies(m, side), side)
        for side in ("xl", "xh"):
            finish_recv(x_copies(m, side), side)
        for q, c in enumerate(Y_COMPS):
            T[m, c, 2:2 + cx, y0 - 2:y0, :] = yr[m, 1, :, 2 * q:2 * q + 2, :]
            T[m, c, 2:2 + cx, y1:y1 + 2, :] = yr[m, 0, :, 2 * q:2 * q + 2, :]
        scale = step_size / (m + 1).astype(F32)

        def edges(g, c_):
            merged = jnp.where(lane % 4 < 2, zr[m, 1, g], zr[m, 0, g])
            for i in range(per):
                for q in range(4):
                    E[q, g * per + i] = pltpu.roll(merged, (2 * cz - (i * 4 + q) * 4 - 2) % cz, 1)
            return c_

        lax.fori_loop(0, cx // per, edges, 0)
        for q in range(4):
            hi, lo = split(E[q].reshape(cx * cy, cz))
            DZ[q] = DZ[q] + (dot16(hi, outer[...]) + dot16(lo, outer[...])).reshape(cx, cy, cz)

        def planes(g, c_):
            for i in range(per):
                px = 2 + g * per + i

                def d_x(c):
                    at = lambda o: T[m, c, px + o, y0:y1, :]
                    return (at(-2) - at(2)) + 8.0 * (at(1) - at(-1))

                def d_y(c):
                    at = lambda o: T[m, c, px, y0 + o:y1 + o, :]
                    return (at(-2) - at(2)) + 8.0 * (at(1) - at(-1))

                def d_z(c):
                    return DZ[Z_COMPS.index(c), px - 2]

                se = inv[px - 2] * scale
                sh = scale / 12.0
                rates = (
                    (d_y(5) - d_z(4)) * se,
                    (d_z(3) - d_x(5)) * se,
                    (d_x(4) - d_y(3)) * se,
                    (d_z(1) - d_y(2)) * sh,
                    (d_x(2) - d_z(0)) * sh,
                    (d_y(0) - d_x(1)) * sh,
                )
                for c in range(6):
                    T[m + 1, c, px, y0:y1, :] = rates[c]
                    F[c, px, y0:y1, :] = F[c, px, y0:y1, :] + rates[c]
            return c_

        lax.fori_loop(0, cx // per, planes, 0)
        return carry

    lax.fori_loop(0, 4, step, 0)

    store = pltpu.make_async_copy(F.at[:, pl.ds(2, cx), pl.ds(8, cy), :], out, load_sem.at[3])
    store.start()

    def xf_copies(side):
        lo_src, lo_dst = (2, cx + 2) if side == "xl" else (cx, 0)
        base = 0 if side == "xl" else 1
        return [remote(F.at[:, pl.ds(lo_src, 2), pl.ds(8, cy)], F.at[:, pl.ds(lo_dst, 2), pl.ds(8, cy)],
                       fsend.at[base], frecv.at[base], dev[side])]

    last = zfs.shape[0] - 1

    def corner_copy(sx, sz):
        kx, kz = (0 if sx == "xl" else 1), (0 if sz == "zl" else 1)
        return remote(zfs.at[0 if sx == "xl" else last], zfd.at[kx, kz],
                      dsend.at[kx * 2 + kz], drecv.at[kx * 2 + kz], corner_dev(sx, sz))

    def yf_copies(side):
        k = 0 if side == "yl" else 1
        return [remote(yfs.at[k], yfr.at[k], fsend.at[4 + k], frecv.at[4 + k], dev[side])]

    def zf_copies(side):
        k = 0 if side == "zl" else 1
        return [remote(zfs, zfr.at[k], fsend.at[6 + k], frecv.at[6 + k], dev[side])]

    for side in ("xl", "xh"):
        start(xf_copies(side), side)
    wide = cz // 32
    for g in range(cx // wide):
        strip = jnp.zeros((cy, cz), F32)
        for i in range(wide):
            for c in range(6):
                b = i * 32 + c * 4
                strip = jnp.where(lane // 4 == b // 4,
                                  pltpu.roll(F[c, 2 + g * wide + i, y0:y1, :], (b + 2) % cz, 1), strip)
        zfs[g] = strip
    for side in ("zl", "zh"):
        start(zf_copies(side), side)
    for sx, sz in corners:
        @pl.when(has[sx] & has[sz])
        def _():
            corner_copy(sx, sz).start()

    for d in range(1, group):
        request(d).wait_recv()
    if cap % 8 == 0:
        served = reqr[...].reshape(slots, 128)
    else:
        served = jnp.concatenate([reqr[o] for o in range(group)], axis=0)
    bx = served[:, 0:1].astype(jnp.int32)
    by = served[:, 1:2].astype(jnp.int32)
    bz = served[:, 2:3].astype(jnp.int32)

    def spread(offset, first):
        total = jnp.zeros(offset.shape, F32)
        for k in range(5):
            total = jnp.where(offset == k, served[:, first + k:first + k + 1], total)
        return total

    yrows = F.shape[2]
    for lo in range(0, W.shape[1], 128):
        li = lo + lax.broadcasted_iota(jnp.int32, (slots, 128), 1)
        both_xy = spread(li // yrows - bx, 3) * spread(li % yrows - 6 - by, 8)
        W[:, lo:lo + 128], W_lo[:, lo:lo + 128] = split(both_xy)
    li = lax.broadcasted_iota(jnp.int32, (slots, cz), 1)
    wz_in[...] = spread(li + 2 - bz, 13)
    tail = li % 4
    wz_halo[...] = jnp.where(li < 24, spread(jnp.where(tail < 2, tail, cz + tail) - bz, 13), 0.0)

    for side in ("zl", "zh"):
        finish_recv(zf_copies(side), side)
    for g in range(cx // wide):
        merged = jnp.where(lane % 4 < 2, zfr[1, g], zfr[0, g])
        for i in range(wide):
            H[2 + g * wide + i, y0:y1, :] = pltpu.roll(merged, (cz - i * 32) % cz, 1) if i else merged
    for sx, sz in corners:
        @pl.when(has[opposite[sx]] & has[opposite[sz]])
        def _():
            corner_copy(sx, sz).wait_recv()
    for kx, at, shift in ((1, 0, (wide - 2) * 32), (0, cx + 2, 0)):
        merged = jnp.where(lane % 4 < 2, zfd[kx, 1], zfd[kx, 0])
        for i in range(2):
            move = (cz - shift - i * 32) % cz
            H[at + i, y0:y1, :] = pltpu.roll(merged, move, 1) if move else merged
    for side in ("xl", "xh"):
        finish_recv(xf_copies(side), side)
    for k, lo in ((0, y0), (1, y1 - 2)):
        for c in range(6):
            yfs[k, :, 2 * c:2 * c + 2, :] = F[c, :, lo:lo + 2, :]
        yfs[k, :, 12:14, :] = H[:, lo:lo + 2, :]
    for side in ("yl", "yh"):
        start(yf_copies(side), side)
    for side in ("yl", "yh"):
        finish_recv(yf_copies(side), side)
    for k, lo in ((1, y0 - 2), (0, y1)):
        for c in range(6):
            F[c, :, lo:lo + 2, :] = yfr[k, :, 2 * c:2 * c + 2, :]
        H[:, lo:lo + 2, :] = yfr[k, :, 12:14, :]

    depth = W.shape[1]

    def apply(block):
        hi, lo = split(block)
        return dot16(W[...], hi) + dot16(W[...], lo) + dot16(W_lo[...], hi)

    halo = apply(H[...].reshape(depth, cz)) * wz_halo[...]
    result = jnp.zeros((slots, cz), F32)
    for c in range(0, 6, 2):
        pair = apply(jnp.concatenate([F[c].reshape(depth, cz), F[c + 1].reshape(depth, cz)], axis=1))
        for k in range(2):
            part = pair[:, k * cz:(k + 1) * cz] * wz_in[...] + jnp.where(li // 4 == c + k, halo, 0.0)
            result = jnp.where(li == c + k, jnp.sum(part, axis=1, keepdims=True), result)
    for o in range(group):
        ans[o] = result[o * cap:(o + 1) * cap]
    for d in range(1, group):
        answer(d).start()
    ansr[me] = ans[me]
    for d in range(1, group):
        answer(d).wait_recv()
    if cap % 8 == 0:
        got = ansr[...].reshape(slots, 128)
    else:
        got = jnp.concatenate([ansr[o] for o in range(group)], axis=0)
    picked = dot(perm[...], got)
    recept[...] = jnp.transpose(picked)[0:6, :]

    store.wait()
    for m in range(4):
        for side in ("xl", "xh"):
            finish_send(x_copies(m, side), side)
        for side in ("yl", "yh"):
            finish_send(y_copies(m, side), side)
        for side in ("zl", "zh"):
            finish_send(z_copies(m, side), side)
    for side in ("xl", "xh"):
        finish_send(xf_copies(side), side)
    for side in ("yl", "yh"):
        finish_send(yf_copies(side), side)
    for side in ("zl", "zh"):
        finish_send(zf_copies(side), side)
    for sx, sz in corners:
        @pl.when(has[sx] & has[sz])
        def _():
            corner_copy(sx, sz).wait_send()
    for d in range(1, group):
        request(d).wait_send()
        answer(d).wait_send()


def local(sizes, fields, permittivity, donor_owner, donor_base, donor_weights):
    nx, ny, nz = sizes
    cx, cy, cz = permittivity.shape
    rows = donor_owner.shape[0]
    group = ny * nz
    cap = 2 * rows // group
    slots = group * cap
    vmem = pltpu.VMEM
    dma = pltpu.SemaphoreType.DMA
    yrows = cy + 16
    depth = (cx + 4) * yrows
    out, recept = pl.pallas_call(
        functools.partial(kernel, (nx, ny, nz, cap)),
        out_shape=(
            jax.ShapeDtypeStruct(fields.shape, F32),
            jax.ShapeDtypeStruct((6, rows), F32),
        ),
        in_specs=[
            pl.BlockSpec(memory_space=pl.ANY),
            pl.BlockSpec(memory_space=pl.ANY),
            pl.BlockSpec(memory_space=vmem),
            pl.BlockSpec(memory_space=vmem),
            pl.BlockSpec(memory_space=vmem),
        ],
        out_specs=(pl.BlockSpec(memory_space=pl.ANY), pl.BlockSpec(memory_space=vmem)),
        scratch_shapes=[
            vmem((5, 6, cx + 4, yrows, cz), F32),
            vmem((6, cx + 4, yrows, cz), F32),
            vmem((cx + 4, yrows, cz), F32),
            vmem((cx, cy, cz), F32),
            vmem((4, 2, cx, 8, cz), F32),
            vmem((4, 2, cx, 8, cz), F32),
            vmem((4, cx * 16 // cz, cy, cz), F32),
            vmem((4, 2, cx * 16 // cz, cy, cz), F32),
            vmem((2, cx + 4, 16, cz), F32),
            vmem((2, cx + 4, 16, cz), F32),
            vmem((cx * 32 // cz, cy, cz), F32),
            vmem((2, cx * 32 // cz, cy, cz), F32),
            vmem((2, 2, cy, cz), F32),
            vmem((4, cx, cy, cz), F32),
            vmem((4, cx, cy, cz), F32),
            vmem((128, rows), F32),
            vmem((cz, cz), jnp.bfloat16),
            vmem((cz, cz), jnp.bfloat16),
            vmem((group, cap, 128), F32),
            vmem((group, cap, 128), F32),
            vmem((group, cap, 128), F32),
            vmem((group, cap, 128), F32),
            vmem((slots, depth), jnp.bfloat16),
            vmem((slots, depth), jnp.bfloat16),
            vmem((slots, cz), F32),
            vmem((slots, cz), F32),
            vmem((rows, slots), F32),
            dma((4,)),
            dma((4, 8)),
            dma((4, 8)),
            dma((8,)),
            dma((8,)),
            dma((group,)),
            dma((group,)),
            dma((group,)),
            dma((group,)),
            dma((4,)),
            dma((4,)),
        ],
        compiler_params=pltpu.CompilerParams(
            collective_id=0, has_side_effects=True, vmem_limit_bytes=40 * 1024 * 1024
        ),
    )(fields, permittivity, donor_owner.T, donor_base.T, donor_weights.T)
    return out, recept


def solution(mesh):
    sizes = (mesh.shape["gx"], mesh.shape["gy"], mesh.shape["gz"])
    placed = (
        P(None, "gx", "gy", "gz"),
        P("gx", "gy", "gz"),
        P(("gx", "gy", "gz"), None),
        P(("gx", "gy", "gz"), None),
        P(("gx", "gy", "gz"), None),
    )
    return jax.shard_map(
        functools.partial(local, sizes),
        mesh=mesh,
        in_specs=placed,
        out_specs=(P(None, "gx", "gy", "gz"), P(None, ("gx", "gy", "gz"))),
        check_vma=False,
    )
```

profile of v0, /device:TPU:0, one launch (start us, length us, event | category | flops | bytes accessed | tf_op | source)
XLA Modules:
  0.0 45.5 jit_solution(9070231925966385643)
XLA Ops:
  0.6 0.0 copy-start.3
  0.6 0.0 copy-start.4
  0.7 0.7 %copy-done.3 = s32[128,3]{0,1:T(4,128)S(1)} copy-done((s32[128,3]{0,1:T(4,128)S(1)}, s32[128,3]{0,1:T(4,128)}, u32[]{:S(2)}) %copy-start.3) | copy-done | bytes 1560
  1.3 0.0 copy-done.4
  1.3 0.0 copy-start
  1.3 1.1 %copy-done = f32[6,16,16,128]{3,2,1,0:T(8,128)S(1)} copy-done((f32[6,16,16,128]{3,2,1,0:T(8,128)S(1)}, f32[6,16,16,128]{3,2,1,0:T(8,128)}, u32[]{:S(2)}) %copy-start) | copy-done | bytes 786456
  2.5 0.0 copy-start.1
  2.5 0.9 %copy-done.1 = f32[16,16,128]{2,1,0:T(8,128)S(1)} copy-done((f32[16,16,128]{2,1,0:T(8,128)S(1)}, f32[16,16,128]{2,1,0:T(8,128)}, u32[]{:S(2)}) %copy-start.1) | copy-done | bytes 131096
  3.4 0.0 copy-start.2
  3.4 0.7 %copy-done.2 = f32[128,15]{0,1:T(8,128)S(1)} copy-done((f32[128,15]{0,1:T(8,128)S(1)}, f32[128,15]{0,1:T(8,128)}, u32[]{:S(2)}) %copy-start.2) | copy-done | bytes 7704
  4.1 40.0 %shard_map.68 = (f32[6,16,16,128]{3,2,1,0:T(8,128)S(1)}, f32[6,128]{1,0:T(8,128)S(1)}) custom-call(f32[6,16,16,128]{3,2,1,0:T(8,128)S(1)} %copy-done, f32[16,16,128]{2,1,0:T(8,128)S(1)} %copy-done.1, s32[1,128]{1,0:T(1,128)S(1)} %bitcast.5, s32[3,128]{1,0:T(4,128)S(1)} %bitcast.4, f32[15,128]{1,0:T(8,128)S(1)} %bitcast.3), custom_call_target="tpu_custom_call" | custom-call | tf_op jit(solution)/shard_map/pallas_call | solution.py:437
  44.0 0.9 %copy.9 = f32[6,16,16,128]{3,2,1,0:T(8,128)} copy(f32[6,16,16,128]{3,2,1,0:T(8,128)S(1)} %get-tuple-element.4) | data formatting | bytes 1572864
  44.9 0.6 %copy.10 = f32[6,128]{1,0:T(8,128)} copy(f32[6,128]{1,0:T(8,128)S(1)} %get-tuple-element.5) | data formatting | bytes 6144
Async XLA Ops:
  0.6 0.7 %copy-start.3 = (s32[128,3]{0,1:T(4,128)S(1)}, s32[128,3]{0,1:T(4,128)}, u32[]{:S(2)}) copy-start(s32[128,3]{0,1:T(4,128)} %param.8) | copy-start | bytes 4612
  0.6 0.7 %copy-start.4 = (s32[128,1]{0,1:T(1,128)S(1)}, s32[128,1]{0,1:T(1,128)}, u32[]{:S(2)}) copy-start(s32[128,1]{0,1:T(1,128)} %param.7) | copy-start | bytes 1540
  1.3 1.1 %copy-start = (f32[6,16,16,128]{3,2,1,0:T(8,128)S(1)}, f32[6,16,16,128]{3,2,1,0:T(8,128)}, u32[]{:S(2)}) copy-start(f32[6,16,16,128]{3,2,1,0:T(8,128)} %fields.1) | copy-start | bytes 2359300
  2.5 0.9 %copy-start.1 = (f32[16,16,128]{2,1,0:T(8,128)S(1)}, f32[16,16,128]{2,1,0:T(8,128)}, u32[]{:S(2)}) copy-start(f32[16,16,128]{2,1,0:T(8,128)} %eps.1) | copy-start | bytes 393220
  3.4 0.7 %copy-start.2 = (f32[128,15]{0,1:T(8,128)S(1)}, f32[128,15]{0,1:T(8,128)}, u32[]{:S(2)}) copy-start(f32[128,15]{0,1:T(8,128)} %param.9) | copy-start | bytes 23044
where the time goes:
time: 45.7 us; the launch traced here: 45.5 us
  Pallas kernels  40 us (88%)
  local copies, waits for them, and re-layouts  4.88 us (11%)
  between operations  0.66 us (1%)
    pallas_call x1, Pallas kernels, local(): pl.pallas_call(functools.partial(kernel, (nx, ny, nz, cap)), out_shape=(j...  40 us
    unnamed x12, local copies, waits for them, and re-layouts  4.88 us

commit v1 on v0

v1 whole, which is shorter than its diff:
```python
import functools

import jax
import jax.numpy as jnp
from jax import lax
from jax.experimental import pallas as pl
from jax.experimental.pallas import tpu as pltpu
from jax.sharding import PartitionSpec as P

step_size = 0.25
MESH = pl.DeviceIdType.MESH
F32 = jnp.float32
BF16 = jnp.bfloat16
HI = lax.Precision.HIGHEST
BLOCKS = 4
FEATURES = 32
DIRS = [(a, b, c) for a in (-1, 0, 1) for b in (-1, 0, 1) for c in (-1, 0, 1) if (a, b, c) != (0, 0, 0)]
FACES = [(-1, 0, 0), (1, 0, 0), (0, -1, 0), (0, 1, 0), (0, 0, -1), (0, 0, 1)]


def dot(a, b, dims=((1,), (0,))):
    return lax.dot_general(a, b, (dims, ((), ())), precision=HI, preferred_element_type=F32)


def split(a):
    hi = a.astype(BF16)
    return hi, (a - hi.astype(F32)).astype(BF16)


def dot16(a, b):
    return lax.dot_general(a, b, (((1,), (0,)), ((), ())), preferred_element_type=F32)


def negate(way):
    return tuple(-a for a in way)


def slot_of(a):
    return 0 if a < 0 else 1


def kernel(
    sizes, fields, eps, owner_in, bases_in, weights_in, out, recept,
    owner, bases, weights, T, F, inv, ys, yr, zs, zr, DZ,
    yfs, zfs, XR, YR, XYR, ZR, ZX, ZY, ZXY,
    data_t, inner, req, reqr, ans, ansr, W, W_lo, V, V_lo, Wy, wzx, wz_in, hits_s, slot_s, part,
    load_sem, send, recv, fsend, frecv, rsend, rrecv, asend, arecv,
):
    nx, ny, nz, cap = sizes
    group = ny * nz
    per_owner = cap // BLOCKS
    cx, cy, cz = eps.shape
    rows = owner.shape[1]
    slots = group * cap
    x, y, z = lax.axis_index("gx"), lax.axis_index("gy"), lax.axis_index("gz")
    me = y * nz + z
    y0, y1 = 8, 8 + cy

    loads = [
        pltpu.make_async_copy(fields, T.at[0, :, pl.ds(2, cx), pl.ds(8, cy), :], load_sem.at[0]),
        pltpu.make_async_copy(owner_in, owner, load_sem.at[1]),
        pltpu.make_async_copy(bases_in, bases, load_sem.at[2]),
        pltpu.make_async_copy(weights_in, weights, load_sem.at[3]),
        pltpu.make_async_copy(eps, inv, load_sem.at[4]),
        pltpu.make_async_copy(fields, F, load_sem.at[5]),
    ]
    for copy in loads:
        copy.start()

    has = {
        (-1, 0, 0): x > 0, (1, 0, 0): x < nx - 1, (0, -1, 0): y > 0,
        (0, 1, 0): y < ny - 1, (0, 0, -1): z > 0, (0, 0, 1): z < nz - 1,
    }
    for way in DIRS:
        found = None
        for axis in range(3):
            if way[axis]:
                face = tuple(way[a] if a == axis else 0 for a in range(3))
                found = has[face] if found is None else found & has[face]
        has[way] = found

    def dev(way):
        return (x + way[0], y + way[1], z + way[2])

    barrier = pltpu.get_barrier_semaphore()
    others = []
    for d in range(1, group):
        t = lax.rem(me + d, group)
        others.append((x, t // nz, lax.rem(t, nz)))
    expected = jnp.int32(group - 1)
    for way in DIRS:
        if way[0]:
            expected = expected + has[way].astype(jnp.int32)

            @pl.when(has[way])
            def _():
                pl.semaphore_signal(barrier, inc=1, device_id=dev(way), device_id_type=MESH)
    for target in others:
        pl.semaphore_signal(barrier, inc=1, device_id=target, device_id_type=MESH)

    def clear(ref):
        ref[...] = jnp.zeros(ref.shape, F32)

    for way in DIRS:
        kx, ky, kz = (slot_of(a) for a in way)
        here = tuple(abs(a) for a in way)

        @pl.when(jnp.logical_not(has[way]))
        def _():
            if here == (1, 0, 0):
                for m in range(4):
                    clear(T.at[m, :, pl.ds(kx * (cx + 2), 2), pl.ds(8, cy)])
                clear(XR.at[:, kx])
            elif here == (0, 1, 0):
                clear(yr.at[:, ky])
                clear(YR.at[:, ky])
            elif here == (0, 0, 1):
                clear(zr.at[:, kz])
                clear(ZR.at[:, kz])
            elif here == (1, 1, 0):
                clear(XYR.at[:, kx, ky])
            elif here == (1, 0, 1):
                clear(ZX.at[:, kx, kz])
            elif here == (0, 1, 1):
                clear(ZY.at[:, ky, kz])
            else:
                clear(ZXY.at[:, kx, ky, kz])

    zi = lax.broadcasted_iota(jnp.int32, (2 * cz, cz), 0) % cz
    zo = lax.broadcasted_iota(jnp.int32, (2 * cz, cz), 1)
    delta = zi - zo
    inner[...] = (jnp.where(delta == -2, 1.0, 0.0) - jnp.where(delta == 2, 1.0, 0.0)
                  + jnp.where(delta == 1, 8.0, 0.0) - jnp.where(delta == -1, 8.0, 0.0)).astype(BF16)

    lane = lax.broadcasted_iota(jnp.int32, (cy, cz), 1)
    lane1 = lax.broadcasted_iota(jnp.int32, (1, cz), 1)

    def remote(src, dst, s, r, target):
        return pltpu.make_async_remote_copy(
            src_ref=src, dst_ref=dst, send_sem=s, recv_sem=r, device_id=target, device_id_type=MESH)

    def request(d):
        return remote(req.at[(me + d) % group], reqr.at[me], rsend.at[d], rrecv.at[d], others[d - 1])

    def answer(d):
        return remote(ans.at[(me + d) % group], ansr.at[me], asend.at[d], arecv.at[d], others[d - 1])

    def parts(h):
        m = h // 2
        sp = (m + h % 2) % 2
        return m, sp, 3 * (1 - sp), 3 * sp

    def face_copy(h, way):
        m, sp, s, d = parts(h)
        i = FACES.index(way)
        if way[0]:
            lo_src, lo_dst = (2, cx + 2) if way[0] < 0 else (cx, 0)
            src = T.at[m, pl.ds(s + 1, 2), pl.ds(lo_src, 2), pl.ds(8, cy)]
            dst = T.at[m, pl.ds(s + 1, 2), pl.ds(lo_dst, 2), pl.ds(8, cy)]
        elif way[1]:
            k = slot_of(way[1])
            src, dst = ys.at[h, k], yr.at[h, 1 - k]
        else:
            src, dst = zs.at[h], zr.at[h, 1 - slot_of(way[2])]
        return remote(src, dst, send.at[h, i], recv.at[h, i], dev(way))

    def start_face(h, ways):
        for way in ways:
            @pl.when(has[way])
            def _():
                face_copy(h, way).start()

    def recv_face(h, ways):
        for way in ways:
            @pl.when(has[negate(way)])
            def _():
                face_copy(h, way).wait_recv()

    XW, YW, ZW = FACES[0:2], FACES[2:4], FACES[4:6]
    per = cz // 8

    def pack_y(h):
        m, sp, s, d = parts(h)
        for q, c in enumerate((0, 2)):
            ys[h, 0, :, 2 * q:2 * q + 2, :] = T[m, s + c, 2:2 + cx, y0:y0 + 2, :]
            ys[h, 1, :, 2 * q:2 * q + 2, :] = T[m, s + c, 2:2 + cx, y1 - 2:y1, :]

    def pack_z(h):
        m, sp, s, d = parts(h)
        for g in range(cx // per):
            strip = jnp.zeros((cy, cz), F32)
            for i in range(per):
                for q in range(2):
                    b = i * 8 + q * 4
                    strip = jnp.where(lane // 4 == b // 4,
                                      pltpu.roll(T[m, s + q, 2 + g * per + i, y0:y1, :], (b + 2) % cz, 1), strip)
            zs[h, g] = strip

    loads[0].wait()
    for h in range(2):
        pack_y(h)
        pack_z(h)
    pl.semaphore_wait(barrier, expected)
    for h in range(2):
        start_face(h, XW + YW + ZW)

    for copy in loads[1:4]:
        copy.wait()
    data_t[...] = jnp.zeros(data_t.shape, F32)
    for b in range(BLOCKS):
        at = b * FEATURES
        data_t[at:at + 3] = bases[...].astype(F32)
        data_t[at + 3:at + 18] = weights[...]
        data_t[at + 18:at + 19] = owner[...].astype(F32)
    data = jnp.transpose(data_t[...])
    col = lax.broadcasted_iota(jnp.int32, (rows, 128), 1)
    own = data[:, 18:19].astype(jnp.int32)
    hits = (own == col).astype(F32)
    hits_s[...] = hits
    earlier = dot16((lax.broadcasted_iota(jnp.int32, (rows, rows), 1)
                     < lax.broadcasted_iota(jnp.int32, (rows, rows), 0)).astype(BF16), hits.astype(BF16))
    slot = jnp.sum(earlier * hits, axis=1, keepdims=True).astype(jnp.int32)
    slot_s[...] = jnp.broadcast_to(slot, slot_s.shape)
    placed = jnp.where(col // FEATURES == slot // per_owner, data, 0.0)
    flat = own * per_owner + slot % per_owner
    perm = (flat == lax.broadcasted_iota(jnp.int32, (rows, group * per_owner), 1)).astype(F32)
    packed = dot(perm, placed, ((0,), (0,)))
    for o in range(group):
        req[o] = packed[o * per_owner:(o + 1) * per_owner]
    reqr[me] = req[me]
    for d in range(1, group):
        request(d).start()

    loads[4].wait()
    inv[...] = 1.0 / (12.0 * inv[...])
    loads[5].wait()

    edge = (lane < 2) | (lane >= cz - 2)
    tail = lane % 4

    def final_copy(j, way):
        i = DIRS.index(way)
        d = 3 * (1 - j)
        here = tuple(abs(a) for a in way)
        kx, ky, kz = (slot_of(a) for a in way)
        nx_, ny_, nz_ = 1 - kx, 1 - ky, 1 - kz
        strip = kx * (zfs.shape[1] - 1)
        if here == (1, 0, 0):
            src, dst = F.at[pl.ds(d, 3), pl.ds(kx * (cx - 2), 2)], XR.at[pl.ds(d, 3), nx_]
        elif here == (0, 1, 0):
            src, dst = yfs.at[j, ky], YR.at[pl.ds(d, 3), ny_]
        elif here == (0, 0, 1):
            src, dst = zfs.at[j], ZR.at[j, nz_]
        elif here == (1, 1, 0):
            src = yfs.at[j, ky, :, pl.ds(kx * (2 * cx - 8), 8)]
            dst = XYR.at[pl.ds(d, 3), nx_, ny_]
        elif here == (1, 0, 1):
            src, dst = zfs.at[j, strip], ZX.at[j, nx_, nz_]
        elif here == (0, 1, 1):
            src, dst = zfs.at[j, :, pl.ds(ky * (cy - 8), 8)], ZY.at[j, ny_, nz_]
        else:
            src, dst = zfs.at[j, strip, pl.ds(ky * (cy - 8), 8)], ZXY.at[j, nx_, ny_, nz_]
        return remote(src, dst, fsend.at[j, i], frecv.at[j, i], dev(way))

    def start_final(j, ways):
        for way in ways:
            @pl.when(has[way])
            def _():
                final_copy(j, way).start()

    wide = cz // 16

    def send_final(j):
        d = 3 * (1 - j)
        start_final(j, XW)
        for k, lo in ((0, 0), (1, cy - 2)):
            for c in range(3):
                for px in range(cx):
                    yfs[j, k, c, 2 * px:2 * px + 2, :] = F[d + c, px, lo:lo + 2, :]
        start_final(j, YW + [way for way in DIRS if way[0] and way[1] and not way[2]])
        for g in range(cx // wide):
            strip = jnp.zeros((cy, cz), F32)
            for i in range(wide):
                for c in range(3):
                    b = i * 16 + c * 4
                    strip = jnp.where(lane // 4 == b // 4,
                                      pltpu.roll(F[d + c, g * wide + i], (b + 2) % cz, 1), strip)
            zfs[j, g] = strip
        start_final(j, [way for way in DIRS if way[2]])

    served_rows = group * per_owner

    def served_table():
        if per_owner % 8 == 0:
            table = reqr[...].reshape(served_rows, 128)
        else:
            table = jnp.concatenate([reqr[o] for o in range(group)], axis=0)
        turned = [table] + [pltpu.roll(table, 128 - b * FEATURES, 1) for b in range(1, BLOCKS)]
        return jnp.concatenate(turned, axis=0)

    def spread(served, at, base, first):
        offset = at - base
        total = jnp.zeros(offset.shape, F32)
        for k in range(5):
            total = jnp.where(offset == k, served[:, first + k:first + k + 1], total)
        return total

    def corner(served, axis):
        return served[:, axis:axis + 1].astype(jnp.int32)

    def build_inner():
        for d in range(1, group):
            request(d).wait_recv()
        served = served_table()
        bx, by = corner(served, 0), corner(served, 1)
        for lo in range(0, cx * cy, 128):
            li = lo + lax.broadcasted_iota(jnp.int32, (1, 128), 1)
            both = spread(served, li // cy + 2, bx, 3) * spread(served, li % cy + 2, by, 8)
            W[:, lo:lo + 128], W_lo[:, lo:lo + 128] = split(both)

    def build_outer():
        served = served_table()
        bx, by = corner(served, 0), corner(served, 1)
        nxr, nyr = 4 * cy, 4 * cx
        for lo in range(0, V.shape[1], 128):
            li = lo + lax.broadcasted_iota(jnp.int32, (1, 128), 1)
            i1 = li % (2 * cy)
            xa = i1 // cy + jnp.where(li >= 2 * cy, cx + 2, 0)
            ya = i1 % cy + 2
            l2 = li - nxr
            xb = (l2 % (2 * cx)) // 2 + 2
            yb = l2 % 2 + jnp.where(l2 >= 2 * cx, cy + 2, 0)
            l3 = li - nxr - nyr
            xc = (l3 % 8) // 2 + jnp.where(l3 >= 16, cx + 2, -2)
            yc = l3 % 2 + jnp.where(l3 % 16 >= 8, cy + 2, 0)
            xe = jnp.where(l2 < 0, xa, jnp.where(l3 < 0, xb, xc))
            ye = jnp.where(l2 < 0, ya, jnp.where(l3 < 0, yb, yc))
            xe = jnp.where(l3 < 32, xe, -8)
            both = spread(served, xe, bx, 3) * spread(served, ye, by, 8)
            n = min(128, V.shape[1] - lo)
            hi, low = split(both)
            V[:, lo:lo + n], V_lo[:, lo:lo + n] = hi[:, 0:n], low[:, 0:n]
        li = lax.broadcasted_iota(jnp.int32, (1, 128), 1)
        ye = jnp.where(li < cy, li + 2, jnp.where(li < cy + 8, li - cy - 6, li - cy - 8 + cy + 2))
        ye = jnp.where(li < cy + 16, ye, -8)
        hi, lo = split(spread(served, ye, by, 8))
        k = cy + 16
        Wy[:, 0:k] = hi[:, 0:k]
        Wy[:, k:2 * k] = hi[:, 0:k]
        Wy[:, 2 * k:3 * k] = lo[:, 0:k]

    def build_z():
        served = served_table()
        bx, bz = corner(served, 0), corner(served, 2)
        wz_in[...] = spread(served, lane1 + 2, bz, 13)
        t = lane1 % 4
        tails = spread(served, jnp.where(t < 2, t, cz + t), bz, 13)
        for g in range(wzx.shape[0]):
            wzx[g] = tails * spread(served, lane1 // 16 + 2 + wide * (g - 1), bx, 3)

    def half(h, carry):
        m, sp, s, d = parts(h)
        hi, lo = split(T[m, pl.ds(s, 2), 2:2 + cx, y0:y1, :].reshape(2 * cx * cy, cz))
        DZ[...] = dot16(jnp.concatenate([hi, lo], axis=1), inner[...]).reshape(2, cx, cy, cz)
        recv_face(h, ZW)
        for g in range(cx // per):
            merged = jnp.where(tail < 2, zr[h, 0, g], zr[h, 1, g])
            l2, r2 = pltpu.roll(merged, cz - 2, 1), pltpu.roll(merged, 2, 1)
            l1, r1 = pltpu.roll(merged, cz - 1, 1), pltpu.roll(merged, 1, 1)
            fix = (jnp.where(tail < 2, -l2, r2)
                   + 8.0 * (jnp.where(tail == 1, l1, 0.0) - jnp.where(tail == 2, r1, 0.0)))
            for i in range(per):
                for q in range(2):
                    b = i * 8 + q * 4
                    DZ[q, g * per + i] = DZ[q, g * per + i] + jnp.where(
                        edge, pltpu.roll(fix, (2 * cz - b - 2) % cz, 1), 0.0)
        recv_face(h, YW)
        for q, c in enumerate((0, 2)):
            T[m, s + c, 2:2 + cx, y0 - 2:y0, :] = yr[h, 0, :, 2 * q:2 * q + 2, :]
            T[m, s + c, 2:2 + cx, y1:y1 + 2, :] = yr[h, 1, :, 2 * q:2 * q + 2, :]
        scale = step_size / (m + 1).astype(F32)
        plain = -scale / 12.0

        def plane(px):
            def d_x(c):
                at = lambda o: T[m, s + c, 2 + px + o, y0:y1, :]
                return (at(-2) - at(2)) + 8.0 * (at(1) - at(-1))

            def d_y(c):
                at = lambda o: T[m, s + c, 2 + px, y0 + o:y1 + o, :]
                return (at(-2) - at(2)) + 8.0 * (at(1) - at(-1))

            by = jnp.where(sp == 0, inv[px] * scale, plain)
            rates = ((d_y(2) - DZ[1, px]) * by, (DZ[0, px] - d_x(2)) * by, (d_x(1) - d_y(0)) * by)
            for c in range(3):
                T[m + 1, d + c, 2 + px, y0:y1, :] = rates[c]
                F[d + c, px] = F[d + c, px] + rates[c]

        for px in range(2, cx - 2):
            plane(px)
        recv_face(h, XW)
        for px in (0, 1, cx - 2, cx - 1):
            plane(px)

        @pl.when(h < 6)
        def _():
            start_face(h + 2, XW)
            pack_y(h + 2)
            start_face(h + 2, YW)
            pack_z(h + 2)
            start_face(h + 2, ZW)

        @pl.when(h >= 6)
        def _():
            send_final(h - 6)

        @pl.when(h == 3)
        def _():
            build_inner()

        @pl.when(h == 4)
        def _():
            build_outer()

        @pl.when(h == 5)
        def _():
            build_z()

        return carry

    lax.fori_loop(0, 8, half, 0)

    store = pltpu.make_async_copy(F, out, load_sem.at[6])
    store.start()

    depth = cx * cy

    def apply(w, w_lo, block):
        hi, lo = split(block)
        return dot16(w[...], hi) + dot16(w[...], lo) + dot16(w_lo[...], hi)

    for c in (3, 4, 5, 0, 1, 2):
        part[c] = apply(W, W_lo, F[c].reshape(depth, cz))

    slot_row = lax.broadcasted_iota(jnp.int32, (slots, cz), 0)
    slot_lane = lax.broadcasted_iota(jnp.int32, (slots, cz), 1)
    place = slot_row // served_rows * per_owner + slot_row % per_owner - slot_lane
    owner_of = slot_lane % 16 // 4
    result = jnp.zeros((slots, cz), F32)
    ktail = lax.broadcasted_iota(jnp.int32, (1, cz), 1) % 4 < 2
    for j in range(2):
        d = 3 * (1 - j)
        for way in [w for w in DIRS if w[2]] + [w for w in DIRS if not w[2]]:
            @pl.when(has[negate(way)])
            def _():
                final_copy(j, way).wait_recv()

        def ring(centre, low, high):
            return jnp.concatenate(
                [jnp.where(ktail, a[0], a[1]) for a in (centre, low, high)], axis=0)

        strips = [ring([ZX[j, 0, k] for k in range(2)], [ZXY[j, 0, 0, k] for k in range(2)],
                       [ZXY[j, 0, 1, k] for k in range(2)])]
        for g in range(cx // wide):
            strips.append(ring([ZR[j, k, g] for k in range(2)], [ZY[j, 0, k, g] for k in range(2)],
                               [ZY[j, 1, k, g] for k in range(2)]))
        strips.append(ring([ZX[j, 1, k] for k in range(2)], [ZXY[j, 1, 0, k] for k in range(2)],
                           [ZXY[j, 1, 1, k] for k in range(2)]))
        hi, lo = split(jnp.concatenate(strips, axis=1))
        zsum = dot16(Wy[...], jnp.concatenate([hi, lo, hi], axis=0))
        zpart = jnp.zeros((slots, cz), F32)
        for g in range(len(strips)):
            zpart = zpart + zsum[:, g * cz:(g + 1) * cz] * wzx[g]
        blocks = []
        for c in range(3):
            pieces = [XR[d + c].reshape(4 * cy, cz), YR[d + c].reshape(4 * cx, cz), XYR[d + c].reshape(32, cz)]
            blocks.append(jnp.concatenate(pieces, axis=0))
        added = apply(V, V_lo, jnp.concatenate(blocks, axis=1))
        for c in range(3):
            both = (part[d + c] + added[:, c * cz:(c + 1) * cz]) * wz_in[...]
            both = both + jnp.where(owner_of == c, zpart, 0.0)
            result = jnp.where(place == -(d + c) * cap, jnp.sum(both, axis=1, keepdims=True), result)

    folded = result[0:served_rows]
    for b in range(1, BLOCKS):
        folded = folded + result[b * served_rows:(b + 1) * served_rows]
    for o in range(group):
        ans[o] = jnp.sum(folded[o * per_owner:(o + 1) * per_owner], axis=0, keepdims=True)
    for d in range(1, group):
        answer(d).start()
    ansr[me] = ans[me]
    sel = lax.broadcasted_iota(jnp.int32, (8, 128), 1) // cap == lax.broadcasted_iota(jnp.int32, (8, 128), 0)
    wanted = lax.broadcasted_iota(jnp.int32, (rows, 128), 1) % cap == slot_s[...]
    for d in range(1, group):
        answer(d).wait_recv()
    got = jnp.concatenate([ansr[o] for o in range(group)], axis=0)
    picked = jnp.where(wanted, dot(hits_s[:, 0:group], got), 0.0)
    recept[...] = dot(sel.astype(F32), picked, ((1,), (1,)))[0:6]

    store.wait()

    def drain(h, carry):
        for way in FACES:
            @pl.when(has[way])
            def _():
                face_copy(h, way).wait_send()
        return carry

    lax.fori_loop(0, 8, drain, 0)
    for j in range(2):
        for way in DIRS:
            @pl.when(has[way])
            def _():
                final_copy(j, way).wait_send()
    for d in range(1, group):
        request(d).wait_send()
        answer(d).wait_send()


def local(sizes, fields, permittivity, donor_owner, donor_base, donor_weights):
    nx, ny, nz = sizes
    cx, cy, cz = permittivity.shape
    rows = donor_owner.shape[0]
    group = ny * nz
    cap = 2 * rows // group
    slots = group * cap
    per_owner = cap // BLOCKS
    vmem = pltpu.VMEM
    dma = pltpu.SemaphoreType.DMA
    yrows = cy + 16
    strips = cx * 8 // cz
    wide = cx * 16 // cz
    outer = 4 * cy + 4 * cx + 32
    out, recept = pl.pallas_call(
        functools.partial(kernel, (nx, ny, nz, cap)),
        out_shape=(
            jax.ShapeDtypeStruct(fields.shape, F32),
            jax.ShapeDtypeStruct((6, rows), F32),
        ),
        in_specs=[pl.BlockSpec(memory_space=pl.ANY)] * 5,
        out_specs=(pl.BlockSpec(memory_space=pl.ANY), pl.BlockSpec(memory_space=vmem)),
        scratch_shapes=[
            vmem((1, rows), jnp.int32),
            vmem((3, rows), jnp.int32),
            vmem((15, rows), F32),
            vmem((5, 6, cx + 4, yrows, cz), F32),
            vmem((6, cx, cy, cz), F32),
            vmem((cx, cy, cz), F32),
            vmem((8, 2, cx, 4, cz), F32),
            vmem((8, 2, cx, 4, cz), F32),
            vmem((8, strips, cy, cz), F32),
            vmem((8, 2, strips, cy, cz), F32),
            vmem((2, cx, cy, cz), F32),
            vmem((2, 2, 3, 2 * cx, cz), F32),
            vmem((2, wide, cy, cz), F32),
            vmem((6, 2, 2, cy, cz), F32),
            vmem((6, 2, 2 * cx, cz), F32),
            vmem((6, 2, 2, 8, cz), F32),
            vmem((2, 2, wide, cy, cz), F32),
            vmem((2, 2, 2, cy, cz), F32),
            vmem((2, 2, 2, wide, 8, cz), F32),
            vmem((2, 2, 2, 2, 8, cz), F32),
            vmem((128, rows), F32),
            vmem((2 * cz, cz), BF16),
            vmem((group, per_owner, 128), F32),
            vmem((group, per_owner, 128), F32),
            vmem((group, 1, 128), F32),
            vmem((group, 1, 128), F32),
            vmem((slots, cx * cy), BF16),
            vmem((slots, cx * cy), BF16),
            vmem((slots, outer), BF16),
            vmem((slots, outer), BF16),
            vmem((slots, 3 * (cy + 16)), BF16),
            vmem((wide + 2, slots, cz), F32),
            vmem((slots, cz), F32),
            vmem((rows, 128), F32),
            vmem((rows, 128), jnp.int32),
            vmem((6, slots, cz), F32),
            dma((8,)),
            dma((8, 6)),
            dma((8, 6)),
            dma((2, 26)),
            dma((2, 26)),
            dma((group,)),
            dma((group,)),
            dma((group,)),
            dma((group,)),
        ],
        compiler_params=pltpu.CompilerParams(
            collective_id=0, has_side_effects=True, vmem_limit_bytes=67043328
        ),
    )(fields, permittivity, donor_owner.T, donor_base.T, donor_weights.T)
    return out, recept


def solution(mesh):
    sizes = (mesh.shape["gx"], mesh.shape["gy"], mesh.shape["gz"])
    placed = (
        P(None, "gx", "gy", "gz"),
        P("gx", "gy", "gz"),
        P(("gx", "gy", "gz"), None),
        P(("gx", "gy", "gz"), None),
        P(("gx", "gy", "gz"), None),
    )
    return jax.shard_map(
        functools.partial(local, sizes),
        mesh=mesh,
        in_specs=placed,
        out_specs=(P(None, "gx", "gy", "gz"), P(None, ("gx", "gy", "gz"))),
        check_vma=False,
    )
```

time: 45.7 us -> 37.4 us (0.82)
  Pallas kernels: 40 us -> 33.9 us
  local copies, waits for them, and re-layouts: 4.88 us -> 2.69 us
    pallas_call x1, Pallas kernels: 40 us -> 33.9 us  [local(): pl.pallas_call(functools.partial(kernel, (nx, ny, nz, cap)), out_shape=(j...]
    unnamed x12 -> x4, local copies, waits for them, and re-layouts: 4.88 us -> 2.69 us
where the time goes in v1:
time: 37.4 us; the launch traced here: 37.3 us
  Pallas kernels  33.9 us (91%)
  local copies, waits for them, and re-layouts  2.69 us (7%)
  between operations  0.65 us (2%)
    pallas_call x1, Pallas kernels, local(): pl.pallas_call(functools.partial(kernel, (nx, ny, nz, cap)), out_shape=(j...  33.9 us
    unnamed x4, local copies, waits for them, and re-layouts  2.69 us

profile of v1, /device:TPU:0, one launch (start us, length us, event | category | flops | bytes accessed | tf_op | source)
XLA Modules:
  0.0 37.3 jit_solution(4628522931062299778)
XLA Ops:
  0.6 33.9 %shard_map.68 = (f32[6,16,16,128]{3,2,1,0:T(8,128)}, f32[6,128]{1,0:T(8,128)}) custom-call(f32[6,16,16,128]{3,2,1,0:T(8,128)} %fields.1, f32[16,16,128]{2,1,0:T(8,128)} %eps.1, s32[1,128]{1,0:T(1,128)} %bitcast.5, s32[3,128]{1,0:T(4,128)} %bitcast.4, f32[15,128]{1,0:T(8,128)} %bitcast.3), custom_call_target="tpu_custom_call" | custom-call | tf_op jit(solution)/shard_map/pallas_call | solution.py:534
  34.5 0.0 copy-start
  34.6 2.1 %copy.9 = f32[6,16,16,128]{3,2,1,0:T(8,128)} copy(f32[6,16,16,128]{3,2,1,0:T(8,128)} %get-tuple-element.4) | data formatting | bytes 1572864
  36.7 0.0 copy-done
  36.7 0.6 %copy.10 = f32[6,128]{1,0:T(8,128)} copy(f32[6,128]{1,0:T(8,128)S(1)} %copy-done) | data formatting | bytes 6144
Async XLA Ops:
  34.5 2.1 %copy-start = (f32[6,128]{1,0:T(8,128)S(1)}, f32[6,128]{1,0:T(8,128)}, u32[]{:S(2)}) copy-start(f32[6,128]{1,0:T(8,128)} %get-tuple-element.5) | copy-start | bytes 9220

commit v2 on v1

--- a/solution.py
+++ b/solution.py
@@ -40,10 +40,10 @@
 
 
 def kernel(
-    sizes, fields, eps, owner_in, bases_in, weights_in, out, recept,
-    owner, bases, weights, T, F, inv, ys, yr, zs, zr, DZ,
+    sizes, W_ring, fields, eps, owner_in, bases_in, weights_in, F, ansr, hits_t, slot_t,
+    owner, bases, weights, T, inv, ys, yr, zs, zr, DZ,
     yfs, zfs, XR, YR, XYR, ZR, ZX, ZY, ZXY,
-    data_t, inner, req, reqr, ans, ansr, W, W_lo, V, V_lo, Wy, wzx, wz_in, hits_s, slot_s, part,
+    data_t, inner, EX, EY, req, reqr, ans, W, W_lo, V, V_lo, Wy, wzx, wz_in, part,
     load_sem, send, recv, fsend, frecv, rsend, rrecv, asend, arecv,
 ):
     nx, ny, nz, cap = sizes
@@ -97,6 +97,78 @@
                 pl.semaphore_signal(barrier, inc=1, device_id=dev(way), device_id_type=MESH)
     for target in others:
         pl.semaphore_signal(barrier, inc=1, device_id=target, device_id_type=MESH)
+
+    lane = lax.broadcasted_iota(jnp.int32, (cy, cz), 1)
+    lane1 = lax.broadcasted_iota(jnp.int32, (1, cz), 1)
+
+    def remote(src, dst, s, r, target):
+        return pltpu.make_async_remote_copy(
+            src_ref=src, dst_ref=dst, send_sem=s, recv_sem=r, device_id=target, device_id_type=MESH)
+
+    def request(d):
+        return remote(req.at[(me + d) % group], reqr.at[me], rsend.at[d], rrecv.at[d], others[d - 1])
+
+    def answer(d):
+        return remote(ans.at[(me + d) % group], ansr.at[me], asend.at[d], arecv.at[d], others[d - 1])
+
+    def parts(h):
+        m = h // 2
+        sp = (m + h % 2) % 2
+        return m, sp, 3 * (1 - sp), 3 * sp
+
+    def face_copy(h, way):
+        m, sp, s, d = parts(h)
+        i = FACES.index(way)
+        if way[0]:
+            lo_src, lo_dst = (2, cx + 2) if way[0] < 0 else (cx, 0)
+            src = T.at[m, pl.ds(s + 1, 2), pl.ds(lo_src, 2), pl.ds(8, cy)]
+            dst = T.at[m, pl.ds(s + 1, 2), pl.ds(lo_dst, 2), pl.ds(8, cy)]
+        elif way[1]:
+            k = slot_of(way[1])
+            src, dst = ys.at[h, k], yr.at[h, 1 - k]
+        else:
+            src, dst = zs.at[h], zr.at[h, 1 - slot_of(way[2])]
+        return remote(src, dst, send.at[h, i], recv.at[h, i], dev(way))
+
+    def start_face(h, ways):
+        for way in ways:
+            @pl.when(has[way])
+            def _():
+                face_copy(h, way).start()
+
+    def recv_face(h, ways):
+        for way in ways:
+            @pl.when(has[negate(way)])
+            def _():
+                face_copy(h, way).wait_recv()
+
+    XW, YW, ZW = FACES[0:2], FACES[2:4], FACES[4:6]
+    per = cz // 8
+
+    def pack_y(h):
+        m, sp, s, d = parts(h)
+        for q, c in enumerate((0, 2)):
+            ys[h, 0, :, 2 * q:2 * q + 2, :] = T[m, s + c, 2:2 + cx, y0:y0 + 2, :]
+            ys[h, 1, :, 2 * q:2 * q + 2, :] = T[m, s + c, 2:2 + cx, y1 - 2:y1, :]
+
+    def pack_z(h):
+        m, sp, s, d = parts(h)
+        for g in range(cx // per):
+            strip = jnp.zeros((cy, cz), F32)
+            for i in range(per):
+                for q in range(2):
+                    b = i * 8 + q * 4
+                    strip = jnp.where(lane // 4 == b // 4,
+                                      pltpu.roll(T[m, s + q, 2 + g * per + i, y0:y1, :], (b + 2) % cz, 1), strip)
+            zs[h, g] = strip
+
+    loads[0].wait()
+    for h in range(2):
+        pack_y(h)
+        pack_z(h)
+    pl.semaphore_wait(barrier, expected)
+    for h in range(2):
+        start_face(h, XW + YW + ZW)
 
     def clear(ref):
         ref[...] = jnp.zeros(ref.shape, F32)
@@ -132,99 +204,26 @@
     inner[...] = (jnp.where(delta == -2, 1.0, 0.0) - jnp.where(delta == 2, 1.0, 0.0)
                   + jnp.where(delta == 1, 8.0, 0.0) - jnp.where(delta == -1, 8.0, 0.0)).astype(BF16)
 
-    lane = lax.broadcasted_iota(jnp.int32, (cy, cz), 1)
-    lane1 = lax.broadcasted_iota(jnp.int32, (1, cz), 1)
-
-    def remote(src, dst, s, r, target):
-        return pltpu.make_async_remote_copy(
-            src_ref=src, dst_ref=dst, send_sem=s, recv_sem=r, device_id=target, device_id_type=MESH)
-
-    def request(d):
-        return remote(req.at[(me + d) % group], reqr.at[me], rsend.at[d], rrecv.at[d], others[d - 1])
-
-    def answer(d):
-        return remote(ans.at[(me + d) % group], ansr.at[me], asend.at[d], arecv.at[d], others[d - 1])
-
-    def parts(h):
-        m = h // 2
-        sp = (m + h % 2) % 2
-        return m, sp, 3 * (1 - sp), 3 * sp
-
-    def face_copy(h, way):
-        m, sp, s, d = parts(h)
-        i = FACES.index(way)
-        if way[0]:
-            lo_src, lo_dst = (2, cx + 2) if way[0] < 0 else (cx, 0)
-            src = T.at[m, pl.ds(s + 1, 2), pl.ds(lo_src, 2), pl.ds(8, cy)]
-            dst = T.at[m, pl.ds(s + 1, 2), pl.ds(lo_dst, 2), pl.ds(8, cy)]
-        elif way[1]:
-            k = slot_of(way[1])
-            src, dst = ys.at[h, k], yr.at[h, 1 - k]
-        else:
-            src, dst = zs.at[h], zr.at[h, 1 - slot_of(way[2])]
-        return remote(src, dst, send.at[h, i], recv.at[h, i], dev(way))
-
-    def start_face(h, ways):
-        for way in ways:
-            @pl.when(has[way])
-            def _():
-                face_copy(h, way).start()
-
-    def recv_face(h, ways):
-        for way in ways:
-            @pl.when(has[negate(way)])
-            def _():
-                face_copy(h, way).wait_recv()
-
-    XW, YW, ZW = FACES[0:2], FACES[2:4], FACES[4:6]
-    per = cz // 8
-
-    def pack_y(h):
-        m, sp, s, d = parts(h)
-        for q, c in enumerate((0, 2)):
-            ys[h, 0, :, 2 * q:2 * q + 2, :] = T[m, s + c, 2:2 + cx, y0:y0 + 2, :]
-            ys[h, 1, :, 2 * q:2 * q + 2, :] = T[m, s + c, 2:2 + cx, y1 - 2:y1, :]
-
-    def pack_z(h):
-        m, sp, s, d = parts(h)
-        for g in range(cx // per):
-            strip = jnp.zeros((cy, cz), F32)
-            for i in range(per):
-                for q in range(2):
-                    b = i * 8 + q * 4
-                    strip = jnp.where(lane // 4 == b // 4,
-                                      pltpu.roll(T[m, s + q, 2 + g * per + i, y0:y1, :], (b + 2) % cz, 1), strip)
-            zs[h, g] = strip
-
-    loads[0].wait()
-    for h in range(2):
-        pack_y(h)
-        pack_z(h)
-    pl.semaphore_wait(barrier, expected)
-    for h in range(2):
-        start_face(h, XW + YW + ZW)
-
     for copy in loads[1:4]:
         copy.wait()
-    data_t[...] = jnp.zeros(data_t.shape, F32)
     for b in range(BLOCKS):
         at = b * FEATURES
         data_t[at:at + 3] = bases[...].astype(F32)
         data_t[at + 3:at + 18] = weights[...]
-        data_t[at + 18:at + 19] = owner[...].astype(F32)
-    data = jnp.transpose(data_t[...])
-    col = lax.broadcasted_iota(jnp.int32, (rows, 128), 1)
-    own = data[:, 18:19].astype(jnp.int32)
-    hits = (own == col).astype(F32)
-    hits_s[...] = hits
-    earlier = dot16((lax.broadcasted_iota(jnp.int32, (rows, rows), 1)
-                     < lax.broadcasted_iota(jnp.int32, (rows, rows), 0)).astype(BF16), hits.astype(BF16))
-    slot = jnp.sum(earlier * hits, axis=1, keepdims=True).astype(jnp.int32)
-    slot_s[...] = jnp.broadcast_to(slot, slot_s.shape)
-    placed = jnp.where(col // FEATURES == slot // per_owner, data, 0.0)
+        data_t[at + 18:at + FEATURES] = jnp.zeros((FEATURES - 18, rows), F32)
+    own = owner[...]
+    hits = jnp.where(lax.broadcasted_iota(jnp.int32, (group, rows), 0) == own, 1.0, 0.0)
+    hits_t[...] = hits
+    earlier = dot16(hits.astype(BF16), (lax.broadcasted_iota(jnp.int32, (rows, rows), 0)
+                                        < lax.broadcasted_iota(jnp.int32, (rows, rows), 1)).astype(BF16))
+    slot_f = jnp.sum(earlier * hits, axis=0, keepdims=True)
+    slot_t[...] = slot_f
+    slot = slot_f.astype(jnp.int32)
+    block = lax.broadcasted_iota(jnp.int32, (BLOCKS * FEATURES, rows), 0) // FEATURES
+    placed = jnp.where(block == slot // per_owner, data_t[...], 0.0)
     flat = own * per_owner + slot % per_owner
-    perm = (flat == lax.broadcasted_iota(jnp.int32, (rows, group * per_owner), 1)).astype(F32)
-    packed = dot(perm, placed, ((0,), (0,)))
+    perm = (flat == lax.broadcasted_iota(jnp.int32, (group * per_owner, rows), 0)).astype(F32)
+    packed = dot(perm, placed, ((1,), (1,)))
     for o in range(group):
         req[o] = packed[o * per_owner:(o + 1) * per_owner]
     reqr[me] = req[me]
@@ -234,6 +233,42 @@
     loads[4].wait()
     inv[...] = 1.0 / (12.0 * inv[...])
     loads[5].wait()
+    here_x = lax.broadcasted_iota(jnp.int32, (64, 128), 0)
+    inside = cx * cy
+    ring_x, ring_y = 4 * cy, 4 * cx
+
+    def one_hot(ref, lo, hot):
+        hot = jnp.where(hot, 1.0, 0.0).astype(BF16)
+        for k in range(3):
+            ref[k * 64:(k + 1) * 64, lo:lo + 128] = hot
+        ref[192:256, lo:lo + 128] = jnp.zeros((64, 128), BF16)
+
+    def place(lo, xe, ye):
+        one_hot(EX, lo, here_x == xe)
+        one_hot(EY, lo, here_x - 32 == ye)
+
+    for lo in range(0, inside, 128):
+        li = lo + lane1
+        place(lo, li // cy + 2, li % cy + 2)
+    for lo in range(0, W_ring, 128):
+        li = lo + lane1
+        i1 = li % (2 * cy)
+        l2 = li - ring_x
+        l3 = li - ring_x - ring_y
+        xe = jnp.where(
+            l2 < 0, i1 // cy + jnp.where(li >= 2 * cy, cx + 2, 0),
+            jnp.where(l3 < 0, (l2 % (2 * cx)) // 2 + 2, (l3 % 8) // 2 + jnp.where(l3 >= 16, cx + 2, -2)))
+        ye = jnp.where(
+            l2 < 0, i1 % cy + 2,
+            jnp.where(l3 < 0, l2 % 2 + jnp.where(l2 >= 2 * cx, cy + 2, 0),
+                      l3 % 2 + jnp.where(l3 % 16 >= 8, cy + 2, 0)))
+        place(inside + lo, jnp.where((l3 < 32) & (xe < 32), xe, -100), jnp.where(l3 < 32, ye, -100))
+    ye = jnp.where(lane1 < cy, lane1 + 2, jnp.where(lane1 < cy + 8, lane1 - cy - 6, lane1 - 6))
+    one_hot(EY, inside + W_ring, here_x - 32 == jnp.where(lane1 < cy + 16, ye, -100))
+    wide = cz // 16
+    for g in range(wzx.shape[0]):
+        xe = lane1 // 16 + 2 + wide * (g - 1)
+        one_hot(EX, inside + W_ring + 128 * g, here_x == jnp.where(xe < 32, xe, -100))
 
     edge = (lane < 2) | (lane >= cz - 2)
     tail = lane % 4
@@ -268,16 +303,9 @@
             def _():
                 final_copy(j, way).start()
 
-    wide = cz // 16
-
     def send_final(j):
         d = 3 * (1 - j)
         start_final(j, XW)
-        for k, lo in ((0, 0), (1, cy - 2)):
-            for c in range(3):
-                for px in range(cx):
-                    yfs[j, k, c, 2 * px:2 * px + 2, :] = F[d + c, px, lo:lo + 2, :]
-        start_final(j, YW + [way for way in DIRS if way[0] and way[1] and not way[2]])
         for g in range(cx // wide):
             strip = jnp.zeros((cy, cz), F32)
             for i in range(wide):
@@ -286,7 +314,12 @@
                     strip = jnp.where(lane // 4 == b // 4,
                                       pltpu.roll(F[d + c, g * wide + i], (b + 2) % cz, 1), strip)
             zfs[j, g] = strip
-        start_final(j, [way for way in DIRS if way[2]])
+        start_final(j, sorted((way for way in DIRS if way[2]), key=lambda way: -sum(map(abs, way))))
+        for k, lo in ((0, 0), (1, cy - 2)):
+            for c in range(3):
+                for px in range(cx):
+                    yfs[j, k, c, 2 * px:2 * px + 2, :] = F[d + c, px, lo:lo + 2, :]
+        start_final(j, [way for way in DIRS if way[0] and way[1] and not way[2]] + YW)
 
     served_rows = group * per_owner
 
@@ -298,70 +331,60 @@
         turned = [table] + [pltpu.roll(table, 128 - b * FEATURES, 1) for b in range(1, BLOCKS)]
         return jnp.concatenate(turned, axis=0)
 
-    def spread(served, at, base, first):
-        offset = at - base
-        total = jnp.zeros(offset.shape, F32)
-        for k in range(5):
-            total = jnp.where(offset == k, served[:, first + k:first + k + 1], total)
-        return total
-
-    def corner(served, axis):
-        return served[:, axis:axis + 1].astype(jnp.int32)
-
-    def build_inner():
+    def build():
         for d in range(1, group):
             request(d).wait_recv()
         served = served_table()
-        bx, by = corner(served, 0), corner(served, 1)
-        for lo in range(0, cx * cy, 128):
-            li = lo + lax.broadcasted_iota(jnp.int32, (1, 128), 1)
-            both = spread(served, li // cy + 2, bx, 3) * spread(served, li % cy + 2, by, 8)
-            W[:, lo:lo + 128], W_lo[:, lo:lo + 128] = split(both)
-
-    def build_outer():
-        served = served_table()
-        bx, by = corner(served, 0), corner(served, 1)
-        nxr, nyr = 4 * cy, 4 * cx
-        for lo in range(0, V.shape[1], 128):
-            li = lo + lax.broadcasted_iota(jnp.int32, (1, 128), 1)
-            i1 = li % (2 * cy)
-            xa = i1 // cy + jnp.where(li >= 2 * cy, cx + 2, 0)
-            ya = i1 % cy + 2
-            l2 = li - nxr
-            xb = (l2 % (2 * cx)) // 2 + 2
-            yb = l2 % 2 + jnp.where(l2 >= 2 * cx, cy + 2, 0)
-            l3 = li - nxr - nyr
-            xc = (l3 % 8) // 2 + jnp.where(l3 >= 16, cx + 2, -2)
-            yc = l3 % 2 + jnp.where(l3 % 16 >= 8, cy + 2, 0)
-            xe = jnp.where(l2 < 0, xa, jnp.where(l3 < 0, xb, xc))
-            ye = jnp.where(l2 < 0, ya, jnp.where(l3 < 0, yb, yc))
-            xe = jnp.where(l3 < 32, xe, -8)
-            both = spread(served, xe, bx, 3) * spread(served, ye, by, 8)
-            n = min(128, V.shape[1] - lo)
-            hi, low = split(both)
-            V[:, lo:lo + n], V_lo[:, lo:lo + n] = hi[:, 0:n], low[:, 0:n]
-        li = lax.broadcasted_iota(jnp.int32, (1, 128), 1)
-        ye = jnp.where(li < cy, li + 2, jnp.where(li < cy + 8, li - cy - 6, li - cy - 8 + cy + 2))
-        ye = jnp.where(li < cy + 16, ye, -8)
-        hi, lo = split(spread(served, ye, by, 8))
+
+        def column(k):
+            return jnp.broadcast_to(served[:, k:k + 1], (slots, 128))
+
+        li = lax.broadcasted_iota(jnp.int32, (slots, 128), 1)
+        flat_lane = li.astype(F32)
+        bx, by, bz = column(0), column(1), column(2)
+        in_x, in_xy = li < 32, li < 64
+        off = jnp.where(in_x, flat_lane - bx, flat_lane - 32.0 - by)
+        t = li % 4
+        off_z = flat_lane + 2.0 - bz
+        off_t = jnp.where(t < 2, t, cz + t).astype(F32) - bz
+        both = jnp.zeros((slots, 128), F32)
+        z_in = jnp.zeros((slots, 128), F32)
+        tails = jnp.zeros((slots, 128), F32)
+        for k in range(5):
+            wz = column(13 + k)
+            both = jnp.where(off == k, jnp.where(in_x, column(3 + k), column(8 + k)), both)
+            z_in = jnp.where(off_z == k, wz, z_in)
+            tails = jnp.where(off_t == k, wz, tails)
+        wz_in[...] = z_in
+        both = jnp.where(in_xy, both, 0.0)
+        hi = both.astype(BF16).astype(F32)
+        mid = (both - hi).astype(BF16).astype(F32)
+        table = jnp.concatenate([(hi + pltpu.roll(mid, 64, 1)).astype(BF16), (both - hi - mid).astype(BF16)], axis=1)
+
+        def weights_at(lo, n):
+            return dot16(table, EX[:, lo:lo + n]) * dot16(table, EY[:, lo:lo + n])
+
+        W[...], W_lo[...] = split(weights_at(0, inside))
+        n = V.shape[1]
+        hi, lo = split(weights_at(inside, W_ring))
+        V[...], V_lo[...] = hi[:, 0:n], lo[:, 0:n]
         k = cy + 16
+        hi, lo = split(dot16(table, EY[:, inside + W_ring:inside + W_ring + 128]))
         Wy[:, 0:k] = hi[:, 0:k]
         Wy[:, k:2 * k] = hi[:, 0:k]
         Wy[:, 2 * k:3 * k] = lo[:, 0:k]
-
-    def build_z():
-        served = served_table()
-        bx, bz = corner(served, 0), corner(served, 2)
-        wz_in[...] = spread(served, lane1 + 2, bz, 13)
-        t = lane1 % 4
-        tails = spread(served, jnp.where(t < 2, t, cz + t), bz, 13)
+        at_x = dot16(table, EX[:, inside + W_ring:])
         for g in range(wzx.shape[0]):
-            wzx[g] = tails * spread(served, lane1 // 16 + 2 + wide * (g - 1), bx, 3)
+            wzx[g] = tails * at_x[:, g * 128:(g + 1) * 128]
 
     def half(h, carry):
         m, sp, s, d = parts(h)
         hi, lo = split(T[m, pl.ds(s, 2), 2:2 + cx, y0:y1, :].reshape(2 * cx * cy, cz))
         DZ[...] = dot16(jnp.concatenate([hi, lo], axis=1), inner[...]).reshape(2, cx, cy, cz)
+        @pl.when(h == 4)
+        def _():
+            build()
+
         recv_face(h, ZW)
         for g in range(cx // per):
             merged = jnp.where(tail < 2, zr[h, 0, g], zr[h, 1, g])
@@ -414,24 +437,9 @@
         def _():
             send_final(h - 6)
 
-        @pl.when(h == 3)
-        def _():
-            build_inner()
-
-        @pl.when(h == 4)
-        def _():
-            build_outer()
-
-        @pl.when(h == 5)
-        def _():
-            build_z()
-
         return carry
 
     lax.fori_loop(0, 8, half, 0)
-
-    store = pltpu.make_async_copy(F, out, load_sem.at[6])
-    store.start()
 
     depth = cx * cy
 
@@ -444,7 +452,7 @@
 
     slot_row = lax.broadcasted_iota(jnp.int32, (slots, cz), 0)
     slot_lane = lax.broadcasted_iota(jnp.int32, (slots, cz), 1)
-    place = slot_row // served_rows * per_owner + slot_row % per_owner - slot_lane
+    target = slot_row // served_rows * per_owner + slot_row % per_owner - slot_lane
     owner_of = slot_lane % 16 // 4
     result = jnp.zeros((slots, cz), F32)
     ktail = lax.broadcasted_iota(jnp.int32, (1, cz), 1) % 4 < 2
@@ -479,7 +487,7 @@
         for c in range(3):
             both = (part[d + c] + added[:, c * cz:(c + 1) * cz]) * wz_in[...]
             both = both + jnp.where(owner_of == c, zpart, 0.0)
-            result = jnp.where(place == -(d + c) * cap, jnp.sum(both, axis=1, keepdims=True), result)
+            result = jnp.where(target == -(d + c) * cap, jnp.sum(both, axis=1, keepdims=True), result)
 
     folded = result[0:served_rows]
     for b in range(1, BLOCKS):
@@ -489,15 +497,6 @@
     for d in range(1, group):
         answer(d).start()
     ansr[me] = ans[me]
-    sel = lax.broadcasted_iota(jnp.int32, (8, 128), 1) // cap == lax.broadcasted_iota(jnp.int32, (8, 128), 0)
-    wanted = lax.broadcasted_iota(jnp.int32, (rows, 128), 1) % cap == slot_s[...]
-    for d in range(1, group):
-        answer(d).wait_recv()
-    got = jnp.concatenate([ansr[o] for o in range(group)], axis=0)
-    picked = jnp.where(wanted, dot(hits_s[:, 0:group], got), 0.0)
-    recept[...] = dot(sel.astype(F32), picked, ((1,), (1,)))[0:6]
-
-    store.wait()
 
     def drain(h, carry):
         for way in FACES:
@@ -514,7 +513,27 @@
                 final_copy(j, way).wait_send()
     for d in range(1, group):
         request(d).wait_send()
+    for d in range(1, group):
+        answer(d).wait_recv()
+    for d in range(1, group):
         answer(d).wait_send()
+
+
+def finish_kernel(cap, F, ansr, hits_t, slot_t, out, recept, sem):
+    store = pltpu.make_async_copy(F, out, sem.at[0])
+    store.start()
+    group = ansr.shape[0]
+    got = jnp.concatenate([ansr[o] for o in range(group)], axis=0)
+    hi, low = split(got)
+    mid, lo = split(got - hi.astype(F32))
+    hits = hits_t[...].astype(BF16)
+    picked = lax.dot_general(jnp.concatenate([hi, mid, lo], axis=0), jnp.concatenate([hits] * 3, axis=0),
+                             (((0,), (0,)), ((), ())), preferred_element_type=F32)
+    at = lax.broadcasted_iota(jnp.int32, picked.shape, 0) % cap
+    picked = jnp.where(at == slot_t[...].astype(jnp.int32), picked, 0.0)
+    for c in range(6):
+        recept[c:c + 1] = jnp.sum(picked[c * cap:(c + 1) * cap], axis=0, keepdims=True)
+    store.wait()
 
 
 def local(sizes, fields, permittivity, donor_owner, donor_base, donor_weights):
@@ -531,20 +550,22 @@
     strips = cx * 8 // cz
     wide = cx * 16 // cz
     outer = 4 * cy + 4 * cx + 32
-    out, recept = pl.pallas_call(
-        functools.partial(kernel, (nx, ny, nz, cap)),
+    ring = -(-outer // 128) * 128
+    new, *answers = pl.pallas_call(
+        functools.partial(kernel, (nx, ny, nz, cap), ring),
         out_shape=(
-            jax.ShapeDtypeStruct(fields.shape, F32),
-            jax.ShapeDtypeStruct((6, rows), F32),
+            vmem(fields.shape, F32),
+            vmem((group, 1, 128), F32),
+            vmem((group, rows), F32),
+            vmem((1, rows), F32),
         ),
         in_specs=[pl.BlockSpec(memory_space=pl.ANY)] * 5,
-        out_specs=(pl.BlockSpec(memory_space=pl.ANY), pl.BlockSpec(memory_space=vmem)),
+        out_specs=(pl.BlockSpec(memory_space=vmem),) * 4,
         scratch_shapes=[
             vmem((1, rows), jnp.int32),
             vmem((3, rows), jnp.int32),
             vmem((15, rows), F32),
             vmem((5, 6, cx + 4, yrows, cz), F32),
-            vmem((6, cx, cy, cz), F32),
             vmem((cx, cy, cz), F32),
             vmem((8, 2, cx, 4, cz), F32),
             vmem((8, 2, cx, 4, cz), F32),
@@ -562,9 +583,10 @@
             vmem((2, 2, 2, 2, 8, cz), F32),
             vmem((128, rows), F32),
             vmem((2 * cz, cz), BF16),
+            vmem((256, cx * cy + ring + 128 * (wide + 2)), BF16),
+            vmem((256, cx * cy + ring + 128), BF16),
             vmem((group, per_owner, 128), F32),
             vmem((group, per_owner, 128), F32),
-            vmem((group, 1, 128), F32),
             vmem((group, 1, 128), F32),
             vmem((slots, cx * cy), BF16),
             vmem((slots, cx * cy), BF16),
@@ -573,8 +595,6 @@
             vmem((slots, 3 * (cy + 16)), BF16),
             vmem((wide + 2, slots, cz), F32),
             vmem((slots, cz), F32),
-            vmem((rows, 128), F32),
-            vmem((rows, 128), jnp.int32),
             vmem((6, slots, cz), F32),
             dma((8,)),
             dma((8, 6)),
@@ -587,10 +607,20 @@
             dma((group,)),
         ],
         compiler_params=pltpu.CompilerParams(
-            collective_id=0, has_side_effects=True, vmem_limit_bytes=67043328
+            collective_id=0, has_side_effects=True, vmem_limit_bytes=60 * 1024 * 1024
         ),
     )(fields, permittivity, donor_owner.T, donor_base.T, donor_weights.T)
-    return out, recept
+    return pl.pallas_call(
+        functools.partial(finish_kernel, cap),
+        out_shape=(
+            jax.ShapeDtypeStruct(fields.shape, F32),
+            jax.ShapeDtypeStruct((6, rows), F32),
+        ),
+        in_specs=[pl.BlockSpec(memory_space=vmem)] * 4,
+        out_specs=(pl.BlockSpec(memory_space=pl.ANY), pl.BlockSpec(memory_space=vmem)),
+        scratch_shapes=[dma((1,))],
+        compiler_params=pltpu.CompilerParams(vmem_limit_bytes=2 * 1024 * 1024),
+    )(new, *answers)
 
 
 def solution(mesh):

time: 37.4 us -> 34.7 us (0.928)
  local copies, waits for them, and re-layouts: 2.69 us -> 0 us
    unnamed x4 -> x0, local copies, waits for them, and re-layouts: 2.69 us -> none
    pallas_call x1 -> x2, Pallas kernels: 33.9 us -> 33.9 us  [the longest x1 32.4 us: local(): pl.pallas_call(functools.partial(kernel, (nx, ny, nz, cap), ring), out_sh...]
where the time goes in v2:
time: 34.7 us; the launch traced here: 34.5 us
  Pallas kernels  33.9 us (98%)
  between operations  0.64 us (2%)
    pallas_call x1, Pallas kernels, local(): pl.pallas_call(functools.partial(kernel, (nx, ny, nz, cap), ring), out_sh...  32.4 us
    pallas_call x1, Pallas kernels, local(): pl.pallas_call(functools.partial(finish_kernel, cap), out_shape=(jax.Shap...  1.48 us

profile of v2, /device:TPU:0, one launch (start us, length us, event | category | flops | bytes accessed | tf_op | source)
XLA Modules:
  0.0 34.5 jit_solution(11990592655493882220)
XLA Ops:
  0.6 32.4 %shard_map.68 = (f32[6,16,16,128]{3,2,1,0:T(8,128)S(1)}, f32[16,1,128]{2,1,0:T(1,128)S(1)}, f32[16,128]{1,0:T(8,128)S(1)}, f32[1,128]{1,0:T(1,128)S(1)}) custom-call(f32[6,16,16,128]{3,2,1,0:T(8,128)} %fields.1, f32[16,16,128]{2,1,0:T(8,128)} %eps.1, s32[1,128]{1,0:T(1,128)} %bitcast.5, s32[3,128]{1,0:T(4,128)} %bitcast.4, f32[15,128]{1,0:T(8,128)} %bitcast.3), custom_call_target="tpu_custom_call" | custom-call | tf_op jit(solution)/shard_map/pallas_call | solution.py:554
  33.1 1.5 %shard_map.69 = (f32[6,16,16,128]{3,2,1,0:T(8,128)}, f32[6,128]{1,0:T(8,128)}) custom-call(f32[6,16,16,128]{3,2,1,0:T(8,128)S(1)} %get-tuple-element.6.F, f32[16,1,128]{2,1,0:T(1,128)S(1)} %get-tuple-element.7.ansr, f32[16,128]{1,0:T(8,128)S(1)} %get-tuple-element.8.hits_t, f32[1,128]{1,0:T(1,128)S(1)} %get-tuple-element.9.slot_t), custom_call_target="tpu_custom_call" | custom-call | tf_op jit(solution)/shard_map/pallas_call | solution.py:613

commit v3 on v2

--- a/solution.py
+++ b/solution.py
@@ -42,9 +42,9 @@
 def kernel(
     sizes, W_ring, fields, eps, owner_in, bases_in, weights_in, F, ansr, hits_t, slot_t,
     owner, bases, weights, T, inv, ys, yr, zs, zr, DZ,
-    yfs, zfs, XR, YR, XYR, ZR, ZX, ZY, ZXY,
-    data_t, inner, EX, EY, req, reqr, ans, W, W_lo, V, V_lo, Wy, wzx, wz_in, part,
-    load_sem, send, recv, fsend, frecv, rsend, rrecv, asend, arecv,
+    yfs, zfs, zys, XR, YR, XYR, ZR, ZX, ZY, ZXY,
+    data_t, inner, gather, EX, EY, req, reqr, ans, W, W_lo, V, V_lo, Wy, wzx, wz_in, part,
+    z_sem, y_sem, load_sem, send, recv, fsend, frecv, rsend, rrecv, asend, arecv,
 ):
     nx, ny, nz, cap = sizes
     group = ny * nz
@@ -64,7 +64,7 @@
         pltpu.make_async_copy(eps, inv, load_sem.at[4]),
         pltpu.make_async_copy(fields, F, load_sem.at[5]),
     ]
-    for copy in loads:
+    for copy in loads[0:5]:
         copy.start()
 
     has = {
@@ -87,16 +87,29 @@
     for d in range(1, group):
         t = lax.rem(me + d, group)
         others.append((x, t // nz, lax.rem(t, nz)))
-    expected = jnp.int32(group - 1)
-    for way in DIRS:
-        if way[0]:
-            expected = expected + has[way].astype(jnp.int32)
-
-            @pl.when(has[way])
-            def _():
-                pl.semaphore_signal(barrier, inc=1, device_id=dev(way), device_id_type=MESH)
-    for target in others:
-        pl.semaphore_signal(barrier, inc=1, device_id=target, device_id_type=MESH)
+    expected = jnp.int32(0)
+    for way in FACES:
+        expected = expected + has[way].astype(jnp.int32)
+
+        @pl.when(has[way])
+        def _():
+            pl.semaphore_signal(barrier, inc=1, device_id=dev(way), device_id_type=MESH)
+
+    def line_stage(k, at, count, sems, up):
+        down = negate(up)
+        for here, side, way in ((at == k, 0, up), (at == count - 1 - k, 1, down)):
+            @pl.when(here)
+            def _():
+                if k > 0:
+                    pl.semaphore_wait(sems.at[side], 1)
+                if k < count - 1:
+                    pl.semaphore_signal(sems.at[side], inc=1, device_id=dev(way), device_id_type=MESH)
+
+    def z_stage(k):
+        line_stage(k, z, nz, z_sem, (0, 0, 1))
+
+    def y_stage(k):
+        line_stage(k, y, ny, y_sem, (0, 1, 0))
 
     lane = lax.broadcasted_iota(jnp.int32, (cy, cz), 1)
     lane1 = lax.broadcasted_iota(jnp.int32, (1, cz), 1)
@@ -163,12 +176,15 @@
             zs[h, g] = strip
 
     loads[0].wait()
+    loads[5].start()
     for h in range(2):
         pack_y(h)
-        pack_z(h)
     pl.semaphore_wait(barrier, expected)
     for h in range(2):
-        start_face(h, XW + YW + ZW)
+        start_face(h, YW + XW)
+        pack_z(h)
+        start_face(h, ZW)
+    z_stage(0)
 
     def clear(ref):
         ref[...] = jnp.zeros(ref.shape, F32)
@@ -188,15 +204,15 @@
                 clear(YR.at[:, ky])
             elif here == (0, 0, 1):
                 clear(zr.at[:, kz])
-                clear(ZR.at[:, kz])
+                clear(ZR.at[kz])
             elif here == (1, 1, 0):
                 clear(XYR.at[:, kx, ky])
             elif here == (1, 0, 1):
-                clear(ZX.at[:, kx, kz])
+                clear(ZX.at[kx, kz])
             elif here == (0, 1, 1):
-                clear(ZY.at[:, ky, kz])
+                clear(ZY.at[ky, kz])
             else:
-                clear(ZXY.at[:, kx, ky, kz])
+                clear(ZXY.at[kx, ky, kz])
 
     zi = lax.broadcasted_iota(jnp.int32, (2 * cz, cz), 0) % cz
     zo = lax.broadcasted_iota(jnp.int32, (2 * cz, cz), 1)
@@ -227,9 +243,6 @@
     for o in range(group):
         req[o] = packed[o * per_owner:(o + 1) * per_owner]
     reqr[me] = req[me]
-    for d in range(1, group):
-        request(d).start()
-
     loads[4].wait()
     inv[...] = 1.0 / (12.0 * inv[...])
     loads[5].wait()
@@ -257,18 +270,23 @@
         l3 = li - ring_x - ring_y
         xe = jnp.where(
             l2 < 0, i1 // cy + jnp.where(li >= 2 * cy, cx + 2, 0),
-            jnp.where(l3 < 0, (l2 % (2 * cx)) // 2 + 2, (l3 % 8) // 2 + jnp.where(l3 >= 16, cx + 2, -2)))
+            jnp.where(l3 < 0, (l2 % (2 * cx)) // 2 + 2, (l3 % 4) // 2 + jnp.where(l3 >= 8, cx + 2, 0)))
         ye = jnp.where(
             l2 < 0, i1 % cy + 2,
             jnp.where(l3 < 0, l2 % 2 + jnp.where(l2 >= 2 * cx, cy + 2, 0),
-                      l3 % 2 + jnp.where(l3 % 16 >= 8, cy + 2, 0)))
-        place(inside + lo, jnp.where((l3 < 32) & (xe < 32), xe, -100), jnp.where(l3 < 32, ye, -100))
-    ye = jnp.where(lane1 < cy, lane1 + 2, jnp.where(lane1 < cy + 8, lane1 - cy - 6, lane1 - 6))
-    one_hot(EY, inside + W_ring, here_x - 32 == jnp.where(lane1 < cy + 16, ye, -100))
-    wide = cz // 16
+                      l3 % 2 + jnp.where(l3 % 8 >= 4, cy + 2, 0)))
+        place(inside + lo, jnp.where(l3 < 16, xe, -100), jnp.where(l3 < 16, ye, -100))
+    ye = jnp.where(lane1 < cy, lane1 + 2, jnp.where(lane1 < cy + 2, lane1 - cy, lane1))
+    one_hot(EY, inside + W_ring, here_x - 32 == jnp.where(lane1 < cy + 4, ye, -100))
+    wide = cz // 32
     for g in range(wzx.shape[0]):
-        xe = lane1 // 16 + 2 + wide * (g - 1)
+        xe = lane1 // 32 + 2 + wide * (g - 1)
         one_hot(EX, inside + W_ring + 128 * g, here_x == jnp.where(xe < 32, xe, -100))
+    comp_row = lax.broadcasted_iota(jnp.int32, (2 * cz, cz), 0) % 32 // 4
+    comp_col = lax.broadcasted_iota(jnp.int32, (2 * cz, cz), 1) // cap
+    gather[...] = jnp.where((comp_row == comp_col) & (comp_row < 6), 1.0, 0.0).astype(BF16)
+    for k in range(1, min(2, nz)):
+        z_stage(k)
 
     edge = (lane < 2) | (lane >= cz - 2)
     tail = lane % 4
@@ -279,22 +297,22 @@
         here = tuple(abs(a) for a in way)
         kx, ky, kz = (slot_of(a) for a in way)
         nx_, ny_, nz_ = 1 - kx, 1 - ky, 1 - kz
-        strip = kx * (zfs.shape[1] - 1)
+        strip = kx * (zfs.shape[0] - 1)
         if here == (1, 0, 0):
             src, dst = F.at[pl.ds(d, 3), pl.ds(kx * (cx - 2), 2)], XR.at[pl.ds(d, 3), nx_]
         elif here == (0, 1, 0):
             src, dst = yfs.at[j, ky], YR.at[pl.ds(d, 3), ny_]
         elif here == (0, 0, 1):
-            src, dst = zfs.at[j], ZR.at[j, nz_]
+            src, dst = zfs, ZR.at[nz_]
         elif here == (1, 1, 0):
-            src = yfs.at[j, ky, :, pl.ds(kx * (2 * cx - 8), 8)]
+            src = yfs.at[j, ky, :, kx * (cx // 2 - 1)]
             dst = XYR.at[pl.ds(d, 3), nx_, ny_]
         elif here == (1, 0, 1):
-            src, dst = zfs.at[j, strip], ZX.at[j, nx_, nz_]
+            src, dst = zfs.at[strip], ZX.at[nx_, nz_]
         elif here == (0, 1, 1):
-            src, dst = zfs.at[j, :, pl.ds(ky * (cy - 8), 8)], ZY.at[j, ny_, nz_]
+            src, dst = zys.at[ky], ZY.at[ny_, nz_]
         else:
-            src, dst = zfs.at[j, strip, pl.ds(ky * (cy - 8), 8)], ZXY.at[j, nx_, ny_, nz_]
+            src, dst = zys.at[ky, strip], ZXY.at[nx_, ny_, nz_]
         return remote(src, dst, fsend.at[j, i], frecv.at[j, i], dev(way))
 
     def start_final(j, ways):
@@ -302,24 +320,6 @@
             @pl.when(has[way])
             def _():
                 final_copy(j, way).start()
-
-    def send_final(j):
-        d = 3 * (1 - j)
-        start_final(j, XW)
-        for g in range(cx // wide):
-            strip = jnp.zeros((cy, cz), F32)
-            for i in range(wide):
-                for c in range(3):
-                    b = i * 16 + c * 4
-                    strip = jnp.where(lane // 4 == b // 4,
-                                      pltpu.roll(F[d + c, g * wide + i], (b + 2) % cz, 1), strip)
-            zfs[j, g] = strip
-        start_final(j, sorted((way for way in DIRS if way[2]), key=lambda way: -sum(map(abs, way))))
-        for k, lo in ((0, 0), (1, cy - 2)):
-            for c in range(3):
-                for px in range(cx):
-                    yfs[j, k, c, 2 * px:2 * px + 2, :] = F[d + c, px, lo:lo + 2, :]
-        start_final(j, [way for way in DIRS if way[0] and way[1] and not way[2]] + YW)
 
     served_rows = group * per_owner
 
@@ -368,7 +368,7 @@
         n = V.shape[1]
         hi, lo = split(weights_at(inside, W_ring))
         V[...], V_lo[...] = hi[:, 0:n], lo[:, 0:n]
-        k = cy + 16
+        k = cy + 8
         hi, lo = split(dot16(table, EY[:, inside + W_ring:inside + W_ring + 128]))
         Wy[:, 0:k] = hi[:, 0:k]
         Wy[:, k:2 * k] = hi[:, 0:k]
@@ -377,13 +377,36 @@
         for g in range(wzx.shape[0]):
             wzx[g] = tails * at_x[:, g * 128:(g + 1) * 128]
 
-    def half(h, carry):
+    z_ways = sorted((way for way in DIRS if way[2]), key=lambda way: -sum(map(abs, way)))
+    flat_ways = [way for way in DIRS if way[0] and way[1] and not way[2]] + YW
+
+    def half(h, last):
         m, sp, s, d = parts(h)
         hi, lo = split(T[m, pl.ds(s, 2), 2:2 + cx, y0:y1, :].reshape(2 * cx * cy, cz))
         DZ[...] = dot16(jnp.concatenate([hi, lo], axis=1), inner[...]).reshape(2, cx, cy, cz)
-        @pl.when(h == 4)
-        def _():
-            build()
+        if not last:
+            @pl.when(h == 1)
+            def _():
+                for k in range(2, min(3, nz)):
+                    z_stage(k)
+
+            @pl.when(h == 2)
+            def _():
+                for k in range(3, nz):
+                    z_stage(k)
+                y_stage(0)
+
+            @pl.when(h == 3)
+            def _():
+                for k in range(1, min(2, ny)):
+                    y_stage(k)
+
+            @pl.when(h == 4)
+            def _():
+                for k in range(2, ny):
+                    y_stage(k)
+                for d in range(1, group):
+                    request(d).start()
 
         recv_face(h, ZW)
         for g in range(cx // per):
@@ -401,8 +424,9 @@
         for q, c in enumerate((0, 2)):
             T[m, s + c, 2:2 + cx, y0 - 2:y0, :] = yr[h, 0, :, 2 * q:2 * q + 2, :]
             T[m, s + c, 2:2 + cx, y1:y1 + 2, :] = yr[h, 1, :, 2 * q:2 * q + 2, :]
-        scale = step_size / (m + 1).astype(F32)
+        scale = step_size / jnp.asarray(m + 1, F32)
         plain = -scale / 12.0
+        strips = [zfs[g] if h == 7 else jnp.zeros((cy, cz), F32) for g in range(cx // wide)] if last else []
 
         def plane(px):
             def d_x(c):
@@ -414,33 +438,56 @@
                 return (at(-2) - at(2)) + 8.0 * (at(1) - at(-1))
 
             by = jnp.where(sp == 0, inv[px] * scale, plain)
-            rates = ((d_y(2) - DZ[1, px]) * by, (DZ[0, px] - d_x(2)) * by, (d_x(1) - d_y(0)) * by)
+            rates = [(d_y(2) - DZ[1, px]) * by, (DZ[0, px] - d_x(2)) * by, (d_x(1) - d_y(0)) * by]
             for c in range(3):
-                T[m + 1, d + c, 2 + px, y0:y1, :] = rates[c]
-                F[d + c, px] = F[d + c, px] + rates[c]
+                total = F[d + c, px] + rates[c]
+                F[d + c, px] = total
+                if last:
+                    rates[c] = total
+                else:
+                    T[m + 1, d + c, 2 + px, y0:y1, :] = rates[c]
+            if last:
+                g, i = px // wide, px % wide
+                for c in range(3):
+                    b = i * 32 + (d + c) * 4
+                    strips[g] = jnp.where(lane // 4 == b // 4, pltpu.roll(rates[c], (b + 2) % cz, 1), strips[g])
 
         for px in range(2, cx - 2):
             plane(px)
         recv_face(h, XW)
         for px in (0, 1, cx - 2, cx - 1):
             plane(px)
-
-        @pl.when(h < 6)
-        def _():
+        if last:
+            j = h - 6
+            for g, strip in enumerate(strips):
+                zfs[g] = strip
+                if j == 1:
+                    zys[0, g] = strip[0:2]
+                    zys[1, g] = strip[cy - 2:cy]
+            if j == 1:
+                start_final(j, z_ways)
+            start_final(j, XW)
+            for k, lo in ((0, 0), (1, cy - 2)):
+                for c in range(3):
+                    for px in range(cx):
+                        yfs[j, k, c, px // 2, px % 2 * 2:px % 2 * 2 + 2, :] = F[d + c, px, lo:lo + 2, :]
+            start_final(j, flat_ways)
+        else:
             start_face(h + 2, XW)
             pack_y(h + 2)
             start_face(h + 2, YW)
             pack_z(h + 2)
             start_face(h + 2, ZW)
 
-        @pl.when(h >= 6)
-        def _():
-            send_final(h - 6)
-
+    def body(h, carry):
+        half(h, False)
         return carry
 
-    lax.fori_loop(0, 8, half, 0)
-
+    lax.fori_loop(0, 6, body, 0)
+    half(6, True)
+    half(7, True)
+
+    build()
     depth = cx * cy
 
     def apply(w, w_lo, block):
@@ -453,41 +500,49 @@
     slot_row = lax.broadcasted_iota(jnp.int32, (slots, cz), 0)
     slot_lane = lax.broadcasted_iota(jnp.int32, (slots, cz), 1)
     target = slot_row // served_rows * per_owner + slot_row % per_owner - slot_lane
-    owner_of = slot_lane % 16 // 4
     result = jnp.zeros((slots, cz), F32)
     ktail = lax.broadcasted_iota(jnp.int32, (1, cz), 1) % 4 < 2
     for j in range(2):
         d = 3 * (1 - j)
-        for way in [w for w in DIRS if w[2]] + [w for w in DIRS if not w[2]]:
+        for way in flat_ways + XW:
             @pl.when(has[negate(way)])
             def _():
                 final_copy(j, way).wait_recv()
 
-        def ring(centre, low, high):
-            return jnp.concatenate(
-                [jnp.where(ktail, a[0], a[1]) for a in (centre, low, high)], axis=0)
-
-        strips = [ring([ZX[j, 0, k] for k in range(2)], [ZXY[j, 0, 0, k] for k in range(2)],
-                       [ZXY[j, 0, 1, k] for k in range(2)])]
-        for g in range(cx // wide):
-            strips.append(ring([ZR[j, k, g] for k in range(2)], [ZY[j, 0, k, g] for k in range(2)],
-                               [ZY[j, 1, k, g] for k in range(2)]))
-        strips.append(ring([ZX[j, 1, k] for k in range(2)], [ZXY[j, 1, 0, k] for k in range(2)],
-                           [ZXY[j, 1, 1, k] for k in range(2)]))
-        hi, lo = split(jnp.concatenate(strips, axis=1))
-        zsum = dot16(Wy[...], jnp.concatenate([hi, lo, hi], axis=0))
-        zpart = jnp.zeros((slots, cz), F32)
-        for g in range(len(strips)):
-            zpart = zpart + zsum[:, g * cz:(g + 1) * cz] * wzx[g]
         blocks = []
         for c in range(3):
-            pieces = [XR[d + c].reshape(4 * cy, cz), YR[d + c].reshape(4 * cx, cz), XYR[d + c].reshape(32, cz)]
+            pieces = ([XR[d + c].reshape(4 * cy, cz)]
+                      + [YR[d + c, k, i] for k in range(2) for i in range(cx // 2)]
+                      + [XYR[d + c, kx, ky] for kx in range(2) for ky in range(2)])
             blocks.append(jnp.concatenate(pieces, axis=0))
         added = apply(V, V_lo, jnp.concatenate(blocks, axis=1))
         for c in range(3):
             both = (part[d + c] + added[:, c * cz:(c + 1) * cz]) * wz_in[...]
-            both = both + jnp.where(owner_of == c, zpart, 0.0)
             result = jnp.where(target == -(d + c) * cap, jnp.sum(both, axis=1, keepdims=True), result)
+
+    for way in z_ways:
+        @pl.when(has[negate(way)])
+        def _():
+            final_copy(1, way).wait_recv()
+
+    def ring(centre, low, high):
+        return jnp.concatenate(
+            [jnp.where(ktail, a[0], a[1]) for a in (centre, low, high)] + [jnp.zeros((4, cz), F32)], axis=0)
+
+    strips = [ring([ZX[0, k] for k in range(2)], [ZXY[0, 0, k] for k in range(2)],
+                   [ZXY[0, 1, k] for k in range(2)])]
+    for g in range(cx // wide):
+        strips.append(ring([ZR[k, g] for k in range(2)], [ZY[0, k, g] for k in range(2)],
+                           [ZY[1, k, g] for k in range(2)]))
+    strips.append(ring([ZX[1, k] for k in range(2)], [ZXY[1, 0, k] for k in range(2)],
+                       [ZXY[1, 1, k] for k in range(2)]))
+    hi, lo = split(jnp.concatenate(strips, axis=1))
+    zsum = dot16(Wy[...], jnp.concatenate([hi, lo, hi], axis=0))
+    zpart = jnp.zeros((slots, cz), F32)
+    for g in range(len(strips)):
+        zpart = zpart + zsum[:, g * cz:(g + 1) * cz] * wzx[g]
+    zsum = dot16(jnp.concatenate(split(zpart), axis=1), gather[...])
+    result = result + jnp.where((target + slot_lane) == slot_lane % cap, zsum, 0.0)
 
     folded = result[0:served_rows]
     for b in range(1, BLOCKS):
@@ -508,9 +563,10 @@
     lax.fori_loop(0, 8, drain, 0)
     for j in range(2):
         for way in DIRS:
-            @pl.when(has[way])
-            def _():
-                final_copy(j, way).wait_send()
+            if j == 1 or not way[2]:
+                @pl.when(has[way])
+                def _():
+                    final_copy(j, way).wait_send()
     for d in range(1, group):
         request(d).wait_send()
     for d in range(1, group):
@@ -519,7 +575,7 @@
         answer(d).wait_send()
 
 
-def finish_kernel(cap, F, ansr, hits_t, slot_t, out, recept, sem):
+def finish_kernel(cap, F, ansr, hits_t, slot_t, out, recept, values, sem):
     store = pltpu.make_async_copy(F, out, sem.at[0])
     store.start()
     group = ansr.shape[0]
@@ -532,8 +588,11 @@
     at = lax.broadcasted_iota(jnp.int32, picked.shape, 0) % cap
     picked = jnp.where(at == slot_t[...].astype(jnp.int32), picked, 0.0)
     for c in range(6):
-        recept[c:c + 1] = jnp.sum(picked[c * cap:(c + 1) * cap], axis=0, keepdims=True)
+        values[c:c + 1] = jnp.sum(picked[c * cap:(c + 1) * cap], axis=0, keepdims=True)
+    small = pltpu.make_async_copy(values, recept, sem.at[1])
+    small.start()
     store.wait()
+    small.wait()
 
 
 def local(sizes, fields, permittivity, donor_owner, donor_base, donor_weights):
@@ -548,8 +607,8 @@
     dma = pltpu.SemaphoreType.DMA
     yrows = cy + 16
     strips = cx * 8 // cz
-    wide = cx * 16 // cz
-    outer = 4 * cy + 4 * cx + 32
+    wide = cx * 32 // cz
+    outer = 4 * cy + 4 * cx + 16
     ring = -(-outer // 128) * 128
     new, *answers = pl.pallas_call(
         functools.partial(kernel, (nx, ny, nz, cap), ring),
@@ -572,16 +631,18 @@
             vmem((8, strips, cy, cz), F32),
             vmem((8, 2, strips, cy, cz), F32),
             vmem((2, cx, cy, cz), F32),
-            vmem((2, 2, 3, 2 * cx, cz), F32),
+            vmem((2, 2, 3, cx // 2, 4, cz), F32),
+            vmem((wide, cy, cz), F32),
+            vmem((2, wide, 2, cz), F32),
+            vmem((6, 2, 2, cy, cz), F32),
+            vmem((6, 2, cx // 2, 4, cz), F32),
+            vmem((6, 2, 2, 4, cz), F32),
             vmem((2, wide, cy, cz), F32),
-            vmem((6, 2, 2, cy, cz), F32),
-            vmem((6, 2, 2 * cx, cz), F32),
-            vmem((6, 2, 2, 8, cz), F32),
-            vmem((2, 2, wide, cy, cz), F32),
-            vmem((2, 2, 2, cy, cz), F32),
-            vmem((2, 2, 2, wide, 8, cz), F32),
-            vmem((2, 2, 2, 2, 8, cz), F32),
+            vmem((2, 2, cy, cz), F32),
+            vmem((2, 2, wide, 2, cz), F32),
+            vmem((2, 2, 2, 2, cz), F32),
             vmem((128, rows), F32),
+            vmem((2 * cz, cz), BF16),
             vmem((2 * cz, cz), BF16),
             vmem((256, cx * cy + ring + 128 * (wide + 2)), BF16),
             vmem((256, cx * cy + ring + 128), BF16),
@@ -592,10 +653,12 @@
             vmem((slots, cx * cy), BF16),
             vmem((slots, outer), BF16),
             vmem((slots, outer), BF16),
-            vmem((slots, 3 * (cy + 16)), BF16),
+            vmem((slots, 3 * (cy + 8)), BF16),
             vmem((wide + 2, slots, cz), F32),
             vmem((slots, cz), F32),
             vmem((6, slots, cz), F32),
+            pltpu.SemaphoreType.REGULAR((2,)),
+            pltpu.SemaphoreType.REGULAR((2,)),
             dma((8,)),
             dma((8, 6)),
             dma((8, 6)),
@@ -617,8 +680,8 @@
             jax.ShapeDtypeStruct((6, rows), F32),
         ),
         in_specs=[pl.BlockSpec(memory_space=vmem)] * 4,
-        out_specs=(pl.BlockSpec(memory_space=pl.ANY), pl.BlockSpec(memory_space=vmem)),
-        scratch_shapes=[dma((1,))],
+        out_specs=(pl.BlockSpec(memory_space=pl.ANY),) * 2,
+        scratch_shapes=[vmem((6, rows), F32), dma((2,))],
         compiler_params=pltpu.CompilerParams(vmem_limit_bytes=2 * 1024 * 1024),
     )(new, *answers)
 

time: 34.7 us -> 32.3 us (0.931)
  Pallas kernels: 33.9 us -> 31.5 us
    pallas_call x1, Pallas kernels: 32.4 us -> 30.6 us  [local(): pl.pallas_call(functools.partial(kernel, (nx, ny, nz, cap), ring), out_sh...]
    pallas_call x1, Pallas kernels: 1.48 us -> 0.9 us  [local(): pl.pallas_call(functools.partial(finish_kernel, cap), out_shape=(jax.Shap...]
where the time goes in v3:
time: 32.3 us; the launch traced here: 32.2 us
  Pallas kernels  31.5 us (98%)
  between operations  0.64 us (2%)
    pallas_call x1, Pallas kernels, local(): pl.pallas_call(functools.partial(kernel, (nx, ny, nz, cap), ring), out_sh...  30.6 us
    pallas_call x1, Pallas kernels, local(): pl.pallas_call(functools.partial(finish_kernel, cap), out_shape=(jax.Shap...  0.9 us

profile of v3, /device:TPU:0, one launch (start us, length us, event | category | flops | bytes accessed | tf_op | source)
XLA Modules:
  0.0 32.2 jit_solution(3216120040722532766)
XLA Ops:
  0.6 30.6 %shard_map.68 = (f32[6,16,16,128]{3,2,1,0:T(8,128)S(1)}, f32[16,1,128]{2,1,0:T(1,128)S(1)}, f32[16,128]{1,0:T(8,128)S(1)}, f32[1,128]{1,0:T(1,128)S(1)}) custom-call(f32[6,16,16,128]{3,2,1,0:T(8,128)} %fields.1, f32[16,16,128]{2,1,0:T(8,128)} %eps.1, s32[1,128]{1,0:T(1,128)} %bitcast.5, s32[3,128]{1,0:T(4,128)} %bitcast.4, f32[15,128]{1,0:T(8,128)} %bitcast.3), custom_call_target="tpu_custom_call" | custom-call | tf_op jit(solution)/shard_map/pallas_call | solution.py:613
  31.3 0.9 %shard_map.69 = (f32[6,16,16,128]{3,2,1,0:T(8,128)}, f32[6,128]{1,0:T(8,128)}) custom-call(f32[6,16,16,128]{3,2,1,0:T(8,128)S(1)} %get-tuple-element.6.F, f32[16,1,128]{2,1,0:T(1,128)S(1)} %get-tuple-element.7.ansr, f32[16,128]{1,0:T(8,128)S(1)} %get-tuple-element.8.hits_t, f32[1,128]{1,0:T(1,128)S(1)} %get-tuple-element.9.slot_t), custom_call_target="tpu_custom_call" | custom-call | tf_op jit(solution)/shard_map/pallas_call | solution.py:676

commit v4 on v3

--- a/solution.py
+++ b/solution.py
@@ -41,9 +41,9 @@
 
 def kernel(
     sizes, W_ring, fields, eps, owner_in, bases_in, weights_in, F, ansr, hits_t, slot_t,
-    owner, bases, weights, T, inv, ys, yr, zs, zr, DZ,
+    owner, bases, weights, T, inv, ys, yr, zs, zr, DZ, R,
     yfs, zfs, zys, XR, YR, XYR, ZR, ZX, ZY, ZXY,
-    data_t, inner, gather, EX, EY, req, reqr, ans, W, W_lo, V, V_lo, Wy, wzx, wz_in, part,
+    data_t, inner, gather, EX, EY, req, reqr, ans, W, V, Wy, wzx, wz_in, part, saved,
     z_sem, y_sem, load_sem, send, recv, fsend, frecv, rsend, rrecv, asend, arecv,
 ):
     nx, ny, nz, cap = sizes
@@ -57,14 +57,15 @@
     y0, y1 = 8, 8 + cy
 
     loads = [
-        pltpu.make_async_copy(fields, T.at[0, :, pl.ds(2, cx), pl.ds(8, cy), :], load_sem.at[0]),
+        pltpu.make_async_copy(fields.at[pl.ds(3, 3)], T.at[0, pl.ds(3, 3), pl.ds(2, cx), pl.ds(8, cy), :], load_sem.at[0]),
         pltpu.make_async_copy(owner_in, owner, load_sem.at[1]),
         pltpu.make_async_copy(bases_in, bases, load_sem.at[2]),
         pltpu.make_async_copy(weights_in, weights, load_sem.at[3]),
         pltpu.make_async_copy(eps, inv, load_sem.at[4]),
         pltpu.make_async_copy(fields, F, load_sem.at[5]),
+        pltpu.make_async_copy(fields.at[pl.ds(0, 3)], T.at[0, pl.ds(0, 3), pl.ds(2, cx), pl.ds(8, cy), :], load_sem.at[6]),
     ]
-    for copy in loads[0:5]:
+    for copy in (loads[0], loads[6], *loads[1:5]):
         copy.start()
 
     has = {
@@ -143,9 +144,9 @@
             src, dst = zs.at[h], zr.at[h, 1 - slot_of(way[2])]
         return remote(src, dst, send.at[h, i], recv.at[h, i], dev(way))
 
-    def start_face(h, ways):
+    def start_face(h, ways, also=None):
         for way in ways:
-            @pl.when(has[way])
+            @pl.when(has[way] if also is None else has[way] & also)
             def _():
                 face_copy(h, way).start()
 
@@ -176,14 +177,18 @@
             zs[h, g] = strip
 
     loads[0].wait()
-    loads[5].start()
-    for h in range(2):
-        pack_y(h)
+    pack_y(0)
     pl.semaphore_wait(barrier, expected)
     for h in range(2):
-        start_face(h, YW + XW)
+        if h == 1:
+            loads[6].wait()
+            loads[5].start()
+            pack_y(h)
+        start_face(h, XW, y % 2 == 0)
+        start_face(h, YW)
         pack_z(h)
         start_face(h, ZW)
+        start_face(h, XW, y % 2 == 1)
     z_stage(0)
 
     def clear(ref):
@@ -315,9 +320,9 @@
             src, dst = zys.at[ky, strip], ZXY.at[nx_, ny_, nz_]
         return remote(src, dst, fsend.at[j, i], frecv.at[j, i], dev(way))
 
-    def start_final(j, ways):
+    def start_final(j, ways, also=None):
         for way in ways:
-            @pl.when(has[way])
+            @pl.when(has[way] if also is None else has[way] & also)
             def _():
                 final_copy(j, way).start()
 
@@ -364,10 +369,13 @@
         def weights_at(lo, n):
             return dot16(table, EX[:, lo:lo + n]) * dot16(table, EY[:, lo:lo + n])
 
-        W[...], W_lo[...] = split(weights_at(0, inside))
-        n = V.shape[1]
+        hi, lo = split(weights_at(0, inside))
+        for k, piece in enumerate((hi, hi, lo)):
+            W[:, k * inside:(k + 1) * inside] = piece
+        n = V.shape[1] // 3
         hi, lo = split(weights_at(inside, W_ring))
-        V[...], V_lo[...] = hi[:, 0:n], lo[:, 0:n]
+        for k, piece in enumerate((hi, hi, lo)):
+            V[:, k * n:(k + 1) * n] = piece[:, 0:n]
         k = cy + 8
         hi, lo = split(dot16(table, EY[:, inside + W_ring:inside + W_ring + 128]))
         Wy[:, 0:k] = hi[:, 0:k]
@@ -408,6 +416,45 @@
                 for d in range(1, group):
                     request(d).start()
 
+        recv_face(h, YW)
+        for q, c in enumerate((0, 2)):
+            T[m, s + c, 2:2 + cx, y0 - 2:y0, :] = yr[h, 0, :, 2 * q:2 * q + 2, :]
+            T[m, s + c, 2:2 + cx, y1:y1 + 2, :] = yr[h, 1, :, 2 * q:2 * q + 2, :]
+        scale = step_size / jnp.asarray(m + 1, F32)
+        plain = -scale / 12.0
+        strips = [zfs[g] if h == 7 else jnp.zeros((cy, cz), F32) for g in range(cx // wide)] if last else []
+
+        def by_of(px):
+            return jnp.where(sp == 0, inv[px] * scale, plain)
+
+        def rates_of(px):
+            def d_x(c):
+                at = lambda o: T[m, s + c, 2 + px + o, y0:y1, :]
+                return (at(-2) - at(2)) + 8.0 * (at(1) - at(-1))
+
+            def d_y(c):
+                at = lambda o: T[m, s + c, 2 + px, y0 + o:y1 + o, :]
+                return (at(-2) - at(2)) + 8.0 * (at(1) - at(-1))
+
+            return [d_y(2) - DZ[1, px], DZ[0, px] - d_x(2), d_x(1) - d_y(0)]
+
+        def finish_plane(px, rates, by, comps=range(3)):
+            for c in comps:
+                rate = rates[c] * by
+                total = F[d + c, px] + rate
+                F[d + c, px] = total
+                if last:
+                    g, i = px // wide, px % wide
+                    b = i * 32 + (d + c) * 4
+                    strips[g] = jnp.where(lane // 4 == b // 4, pltpu.roll(total, (b + 2) % cz, 1), strips[g])
+                else:
+                    T[m + 1, d + c, 2 + px, y0:y1, :] = rate
+
+        for px in range(2, cx - 2):
+            rates = rates_of(px)
+            for c in range(2):
+                R[c, px] = rates[c]
+            finish_plane(px, rates, by_of(px), (2,))
         recv_face(h, ZW)
         for g in range(cx // per):
             merged = jnp.where(tail < 2, zr[h, 0, g], zr[h, 1, g])
@@ -415,48 +462,20 @@
             l1, r1 = pltpu.roll(merged, cz - 1, 1), pltpu.roll(merged, 1, 1)
             fix = (jnp.where(tail < 2, -l2, r2)
                    + 8.0 * (jnp.where(tail == 1, l1, 0.0) - jnp.where(tail == 2, r1, 0.0)))
-            for i in range(per):
-                for q in range(2):
-                    b = i * 8 + q * 4
-                    DZ[q, g * per + i] = DZ[q, g * per + i] + jnp.where(
-                        edge, pltpu.roll(fix, (2 * cz - b - 2) % cz, 1), 0.0)
-        recv_face(h, YW)
-        for q, c in enumerate((0, 2)):
-            T[m, s + c, 2:2 + cx, y0 - 2:y0, :] = yr[h, 0, :, 2 * q:2 * q + 2, :]
-            T[m, s + c, 2:2 + cx, y1:y1 + 2, :] = yr[h, 1, :, 2 * q:2 * q + 2, :]
-        scale = step_size / jnp.asarray(m + 1, F32)
-        plain = -scale / 12.0
-        strips = [zfs[g] if h == 7 else jnp.zeros((cy, cz), F32) for g in range(cx // wide)] if last else []
-
-        def plane(px):
-            def d_x(c):
-                at = lambda o: T[m, s + c, 2 + px + o, y0:y1, :]
-                return (at(-2) - at(2)) + 8.0 * (at(1) - at(-1))
-
-            def d_y(c):
-                at = lambda o: T[m, s + c, 2 + px, y0 + o:y1 + o, :]
-                return (at(-2) - at(2)) + 8.0 * (at(1) - at(-1))
-
-            by = jnp.where(sp == 0, inv[px] * scale, plain)
-            rates = [(d_y(2) - DZ[1, px]) * by, (DZ[0, px] - d_x(2)) * by, (d_x(1) - d_y(0)) * by]
-            for c in range(3):
-                total = F[d + c, px] + rates[c]
-                F[d + c, px] = total
-                if last:
-                    rates[c] = total
+
+            def at_edge(px, q):
+                b = px % per * 8 + q * 4
+                return jnp.where(edge, pltpu.roll(fix, (2 * cz - b - 2) % cz, 1), 0.0)
+
+            for px in range(g * per, (g + 1) * per):
+                if px in (0, 1, cx - 2, cx - 1):
+                    for q in range(2):
+                        DZ[q, px] = DZ[q, px] + at_edge(px, q)
                 else:
-                    T[m + 1, d + c, 2 + px, y0:y1, :] = rates[c]
-            if last:
-                g, i = px // wide, px % wide
-                for c in range(3):
-                    b = i * 32 + (d + c) * 4
-                    strips[g] = jnp.where(lane // 4 == b // 4, pltpu.roll(rates[c], (b + 2) % cz, 1), strips[g])
-
-        for px in range(2, cx - 2):
-            plane(px)
+                    finish_plane(px, [R[0, px] - at_edge(px, 1), R[1, px] + at_edge(px, 0)], by_of(px), (0, 1))
         recv_face(h, XW)
         for px in (0, 1, cx - 2, cx - 1):
-            plane(px)
+            finish_plane(px, rates_of(px), by_of(px))
         if last:
             j = h - 6
             for g, strip in enumerate(strips):
@@ -466,18 +485,20 @@
                     zys[1, g] = strip[cy - 2:cy]
             if j == 1:
                 start_final(j, z_ways)
-            start_final(j, XW)
+            start_final(j, XW, y % 2 == 0)
             for k, lo in ((0, 0), (1, cy - 2)):
                 for c in range(3):
                     for px in range(cx):
                         yfs[j, k, c, px // 2, px % 2 * 2:px % 2 * 2 + 2, :] = F[d + c, px, lo:lo + 2, :]
             start_final(j, flat_ways)
+            start_final(j, XW, y % 2 == 1)
         else:
-            start_face(h + 2, XW)
+            start_face(h + 2, XW, y % 2 == 0)
             pack_y(h + 2)
             start_face(h + 2, YW)
             pack_z(h + 2)
             start_face(h + 2, ZW)
+            start_face(h + 2, XW, y % 2 == 1)
 
     def body(h, carry):
         half(h, False)
@@ -490,45 +511,47 @@
     build()
     depth = cx * cy
 
-    def apply(w, w_lo, block):
+    def apply(w, block):
         hi, lo = split(block)
-        return dot16(w[...], hi) + dot16(w[...], lo) + dot16(w_lo[...], hi)
-
-    for c in (3, 4, 5, 0, 1, 2):
-        part[c] = apply(W, W_lo, F[c].reshape(depth, cz))
+        return dot16(w[...], jnp.concatenate([hi, lo, hi], axis=0))
+
+    for d in (3, 0):
+        both = apply(W, jnp.concatenate([F[d + c].reshape(depth, cz) for c in range(3)], axis=1))
+        for c in range(3):
+            part[d + c] = both[:, c * cz:(c + 1) * cz]
 
     slot_row = lax.broadcasted_iota(jnp.int32, (slots, cz), 0)
     slot_lane = lax.broadcasted_iota(jnp.int32, (slots, cz), 1)
     target = slot_row // served_rows * per_owner + slot_row % per_owner - slot_lane
     result = jnp.zeros((slots, cz), F32)
     ktail = lax.broadcasted_iota(jnp.int32, (1, cz), 1) % 4 < 2
-    for j in range(2):
+    def faces(j, result):
         d = 3 * (1 - j)
-        for way in flat_ways + XW:
-            @pl.when(has[negate(way)])
-            def _():
-                final_copy(j, way).wait_recv()
-
         blocks = []
         for c in range(3):
             pieces = ([XR[d + c].reshape(4 * cy, cz)]
                       + [YR[d + c, k, i] for k in range(2) for i in range(cx // 2)]
                       + [XYR[d + c, kx, ky] for kx in range(2) for ky in range(2)])
             blocks.append(jnp.concatenate(pieces, axis=0))
-        added = apply(V, V_lo, jnp.concatenate(blocks, axis=1))
+        added = apply(V, jnp.concatenate(blocks, axis=1))
         for c in range(3):
             both = (part[d + c] + added[:, c * cz:(c + 1) * cz]) * wz_in[...]
             result = jnp.where(target == -(d + c) * cap, jnp.sum(both, axis=1, keepdims=True), result)
-
-    for way in z_ways:
-        @pl.when(has[negate(way)])
-        def _():
-            final_copy(1, way).wait_recv()
+        return result
+
+    def recv_final(j, ways):
+        for way in ways:
+            @pl.when(has[negate(way)])
+            def _():
+                final_copy(j, way).wait_recv()
 
     def ring(centre, low, high):
         return jnp.concatenate(
             [jnp.where(ktail, a[0], a[1]) for a in (centre, low, high)] + [jnp.zeros((4, cz), F32)], axis=0)
 
+    recv_final(0, flat_ways + XW)
+    saved[...] = faces(0, result)
+    recv_final(1, flat_ways + XW + z_ways)
     strips = [ring([ZX[0, k] for k in range(2)], [ZXY[0, 0, k] for k in range(2)],
                    [ZXY[0, 1, k] for k in range(2)])]
     for g in range(cx // wide):
@@ -542,6 +565,7 @@
     for g in range(len(strips)):
         zpart = zpart + zsum[:, g * cz:(g + 1) * cz] * wzx[g]
     zsum = dot16(jnp.concatenate(split(zpart), axis=1), gather[...])
+    result = faces(1, saved[...])
     result = result + jnp.where((target + slot_lane) == slot_lane % cap, zsum, 0.0)
 
     folded = result[0:served_rows]
@@ -631,6 +655,7 @@
             vmem((8, strips, cy, cz), F32),
             vmem((8, 2, strips, cy, cz), F32),
             vmem((2, cx, cy, cz), F32),
+            vmem((2, cx, cy, cz), F32),
             vmem((2, 2, 3, cx // 2, 4, cz), F32),
             vmem((wide, cy, cz), F32),
             vmem((2, wide, 2, cz), F32),
@@ -649,14 +674,13 @@
             vmem((group, per_owner, 128), F32),
             vmem((group, per_owner, 128), F32),
             vmem((group, 1, 128), F32),
-            vmem((slots, cx * cy), BF16),
-            vmem((slots, cx * cy), BF16),
-            vmem((slots, outer), BF16),
-            vmem((slots, outer), BF16),
+            vmem((slots, 3 * cx * cy), BF16),
+            vmem((slots, 3 * outer), BF16),
             vmem((slots, 3 * (cy + 8)), BF16),
             vmem((wide + 2, slots, cz), F32),
             vmem((slots, cz), F32),
             vmem((6, slots, cz), F32),
+            vmem((slots, cz), F32),
             pltpu.SemaphoreType.REGULAR((2,)),
             pltpu.SemaphoreType.REGULAR((2,)),
             dma((8,)),

time: 32.3 us -> 31.2 us (0.966)
  Pallas kernels: 31.5 us -> 30.4 us
    pallas_call x1, Pallas kernels: 30.6 us -> 29.5 us  [local(): pl.pallas_call(functools.partial(kernel, (nx, ny, nz, cap), ring), out_sh...]
where the time goes in v4:
time: 31.2 us; the launch traced here: 31 us
  Pallas kernels  30.4 us (97%)
  between operations  0.64 us (2%)
    pallas_call x1, Pallas kernels, local(): pl.pallas_call(functools.partial(kernel, (nx, ny, nz, cap), ring), out_sh...  29.5 us
    pallas_call x1, Pallas kernels, local(): pl.pallas_call(functools.partial(finish_kernel, cap), out_shape=(jax.Shap...  0.9 us

profile of v4, /device:TPU:0, one launch (start us, length us, event | category | flops | bytes accessed | tf_op | source)
XLA Modules:
  0.0 31.0 jit_solution(4675907787875365177)
XLA Ops:
  0.6 29.5 %shard_map.68 = (f32[6,16,16,128]{3,2,1,0:T(8,128)S(1)}, f32[16,1,128]{2,1,0:T(1,128)S(1)}, f32[16,128]{1,0:T(8,128)S(1)}, f32[1,128]{1,0:T(1,128)S(1)}) custom-call(f32[6,16,16,128]{3,2,1,0:T(8,128)} %fields.1, f32[16,16,128]{2,1,0:T(8,128)} %eps.1, s32[1,128]{1,0:T(1,128)} %bitcast.5, s32[3,128]{1,0:T(4,128)} %bitcast.4, f32[15,128]{1,0:T(8,128)} %bitcast.3), custom_call_target="tpu_custom_call" | custom-call | tf_op jit(solution)/shard_map/pallas_call | solution.py:637
  30.1 0.9 %shard_map.69 = (f32[6,16,16,128]{3,2,1,0:T(8,128)}, f32[6,128]{1,0:T(8,128)}) custom-call(f32[6,16,16,128]{3,2,1,0:T(8,128)S(1)} %get-tuple-element.6.F, f32[16,1,128]{2,1,0:T(1,128)S(1)} %get-tuple-element.7.ansr, f32[16,128]{1,0:T(8,128)S(1)} %get-tuple-element.8.hits_t, f32[1,128]{1,0:T(1,128)S(1)} %get-tuple-element.9.slot_t), custom_call_target="tpu_custom_call" | custom-call | tf_op jit(solution)/shard_map/pallas_call | solution.py:700

commit v5 on v4

--- a/solution.py
+++ b/solution.py
@@ -551,7 +551,7 @@
 
     recv_final(0, flat_ways + XW)
     saved[...] = faces(0, result)
-    recv_final(1, flat_ways + XW + z_ways)
+    recv_final(1, z_ways)
     strips = [ring([ZX[0, k] for k in range(2)], [ZXY[0, 0, k] for k in range(2)],
                    [ZXY[0, 1, k] for k in range(2)])]
     for g in range(cx // wide):
@@ -565,8 +565,9 @@
     for g in range(len(strips)):
         zpart = zpart + zsum[:, g * cz:(g + 1) * cz] * wzx[g]
     zsum = dot16(jnp.concatenate(split(zpart), axis=1), gather[...])
-    result = faces(1, saved[...])
-    result = result + jnp.where((target + slot_lane) == slot_lane % cap, zsum, 0.0)
+    saved[...] = saved[...] + jnp.where((target + slot_lane) == slot_lane % cap, zsum, 0.0)
+    recv_final(1, flat_ways + XW)
+    result = saved[...] + faces(1, result)
 
     folded = result[0:served_rows]
     for b in range(1, BLOCKS):

time: 31.2 us -> 31.3 us (level)
  no operation moved by 1% of the time
where the time goes in v5:
time: 31.3 us; the launch traced here: 31.1 us
  Pallas kernels  30.5 us (97%)
  between operations  0.64 us (2%)
    pallas_call x1, Pallas kernels, local(): pl.pallas_call(functools.partial(kernel, (nx, ny, nz, cap), ring), out_sh...  29.6 us
    pallas_call x1, Pallas kernels, local(): pl.pallas_call(functools.partial(finish_kernel, cap), out_shape=(jax.Shap...  0.9 us

profile of v5, /device:TPU:0, one launch (start us, length us, event | category | flops | bytes accessed | tf_op | source)
XLA Modules:
  0.0 31.1 jit_solution(16798300808914836274)
XLA Ops:
  0.6 29.6 %shard_map.68 = (f32[6,16,16,128]{3,2,1,0:T(8,128)S(1)}, f32[16,1,128]{2,1,0:T(1,128)S(1)}, f32[16,128]{1,0:T(8,128)S(1)}, f32[1,128]{1,0:T(1,128)S(1)}) custom-call(f32[6,16,16,128]{3,2,1,0:T(8,128)} %fields.1, f32[16,16,128]{2,1,0:T(8,128)} %eps.1, s32[1,128]{1,0:T(1,128)} %bitcast.5, s32[3,128]{1,0:T(4,128)} %bitcast.4, f32[15,128]{1,0:T(8,128)} %bitcast.3), custom_call_target="tpu_custom_call" | custom-call | tf_op jit(solution)/shard_map/pallas_call | solution.py:638
  30.2 0.9 %shard_map.69 = (f32[6,16,16,128]{3,2,1,0:T(8,128)}, f32[6,128]{1,0:T(8,128)}) custom-call(f32[6,16,16,128]{3,2,1,0:T(8,128)S(1)} %get-tuple-element.6.F, f32[16,1,128]{2,1,0:T(1,128)S(1)} %get-tuple-element.7.ansr, f32[16,128]{1,0:T(8,128)S(1)} %get-tuple-element.8.hits_t, f32[1,128]{1,0:T(1,128)S(1)} %get-tuple-element.9.slot_t), custom_call_target="tpu_custom_call" | custom-call | tf_op jit(solution)/shard_map/pallas_call | solution.py:701
